TPU v7x, 1024 devices: a whole 8x8x8 slice. The times are simulated.
1024 devices in a mesh: mem: 16 (over x_lo, y), band: 64 (over x_hi, z, core).
Axes of the slice: x: 8 (x_hi: 4, x_lo: 2; x = x_hi * 2 + x_lo), y: 8, z: 8, core: 2. Of those that a mesh axis runs over, the one named last changes fastest.
Arguments:
- ensemble: float32 [64, 4, 256, 1440], P('mem', None, 'band'), may hold values from -6 to 6
- gradient: float32 [4, 1024, 5760], P(None, 'band', 'mem'), may hold values from -60 to 60
- previous: float32 [4, 1024, 5760], P(None, 'band', 'mem'), may hold values from -6 to 6
- diffusivity: float32 [4, 1024, 5760], P(None, 'band', 'mem'), may hold values from 0.03 to 0.12
Outputs:
- analysis: float32 [4, 1024, 5760], P(None, 'band', 'mem')
- direction: float32 [4, 1024, 5760], P(None, 'band', 'mem')
All inputs are finite; a program needn't handle non-finite values.
Results may differ from a plain program's by a relative error of at most 0.00012.
Values sent between devices are 32-bit elements; how exact they have to be, the bound alone decides.
No kernel may reach another device: no remote copies, remote signals or barrier semaphores. Data moves between devices by JAX's collectives and lax.ppermute only.
A program may use at most 64 MiB of HBM per device.

v0:
```python
import jax
import jax.numpy as jnp
from jax import lax
from jax.sharding import Mesh
from jax.sharding import PartitionSpec as P

NLON = 1440
REFINE = 4
SUBSTEPS = 16
LSTEPS = 4
LOCLON = 48
BAND = ("band_0", "band_1", "band_2")
MEM_BAND = ("mem_0", "mem_1", "band_0", "band_1", "band_2")
MEM = ("mem_0", "mem_1")


LATITUDE_RATE = 0.25
HYBRID_WEIGHT = 0.5


def padded(block, sides, width, periodic):
    for axis, dim in sides:
        count = lax.axis_size(axis)
        forward = [(i, i + 1) for i in range(count - 1)]
        if periodic:
            forward.append((count - 1, 0))
        backward = [(target, source) for source, target in forward]
        low = lax.ppermute(
            lax.slice_in_dim(block, block.shape[dim] - width, None, axis=dim), axis, forward
        )
        high = lax.ppermute(lax.slice_in_dim(block, 0, width, axis=dim), axis, backward)
        block = jnp.concatenate([low, block, high], axis=dim)
    return block


def from_everyone(shard, axis):
    copies = jnp.broadcast_to(shard, (lax.axis_size(axis), *shard.shape))
    return lax.all_to_all(copies, axis, split_axis=0, concat_axis=0, tiled=True)


def joined_along(blocks, dim):
    shape = list(blocks.shape[1:])
    shape[dim] *= blocks.shape[0]
    return jnp.moveaxis(blocks, 0, dim).reshape(shape)


def gather_directly(shard, axis, dim):
    blocks = from_everyone(shard, axis)
    return joined_along(blocks, dim)


def split_up(shard, dim, devices):
    before, after = (shard.shape[:dim], shard.shape[dim + 1 :])
    return jnp.moveaxis(shard.reshape(*before, devices, -1, *after), dim, 0)


def sum_at_owner(shard, axis, dim):
    blocks = split_up(shard, dim, lax.axis_size(axis))
    arrived = lax.all_to_all(blocks, axis, split_axis=0, concat_axis=0, tiled=True)
    return arrived.sum(axis=0)


def one_axis_at_a_time(shard, axes):
    for axis in axes:
        shard = lax.psum(shard, axis)
    return shard


def longitude_kernel(extent, length):
    places = jnp.arange(extent, dtype=jnp.float32)
    spacing = jnp.abs(places[:, None] - places[None, :])
    spacing = jnp.minimum(spacing, extent - spacing)
    return jnp.exp(-0.5 * (spacing / length) ** 2)


def fine_faces(padded_rate, first_row, total_rows):
    height = padded_rate.shape[1]
    east_faces = jnp.sqrt(padded_rate[:, :, :-1] * padded_rate[:, :, 1:])
    north_faces = jnp.sqrt(padded_rate[:, :-1, :] * padded_rate[:, 1:, :])
    global_rows = first_row + jnp.arange(height - 1, dtype=jnp.int32)
    inside = (global_rows >= 0) & (global_rows + 1 <= total_rows - 1)
    north_faces = jnp.where(inside[None, :, None], north_faces, jnp.zeros_like(north_faces))
    return (east_faces, north_faces)


def fine_substep(extended, east_faces, north_faces, offset):
    height = extended.shape[1]
    breadth = extended.shape[2]
    low_row = offset + 1
    high_row = low_row + height - 2
    low_col = offset + 1
    high_col = low_col + breadth - 2
    center = extended[:, 1:-1, 1:-1]
    east_face = east_faces[:, low_row:high_row, low_col:high_col]
    west_face = east_faces[:, low_row:high_row, low_col - 1 : high_col - 1]
    north_face = north_faces[:, low_row:high_row, low_col:high_col]
    south_face = north_faces[:, low_row - 1 : high_row - 1, low_col:high_col]
    change = east_face * (extended[:, 1:-1, 2:] - center) + west_face * (
        extended[:, 1:-1, :-2] - center
    )
    change = (
        change
        + north_face * (extended[:, 2:, 1:-1] - center)
        + south_face * (extended[:, :-2, 1:-1] - center)
    )
    return center + change


def localize(control, kernel, band_index, total_coarse):
    members, coarse_rows, columns = control.shape
    blended = jnp.dot(
        control.reshape(members * coarse_rows, columns), kernel, precision=lax.Precision.HIGHEST
    ).reshape(members, coarse_rows, columns)
    extended = padded(blended, ((BAND, 1),), LSTEPS, False)
    ext_rows = coarse_rows + 2 * LSTEPS
    global_rows = band_index * coarse_rows - LSTEPS + jnp.arange(ext_rows - 1, dtype=jnp.int32)
    inside = (global_rows >= 0) & (global_rows + 1 <= total_coarse - 1)
    face_rate = jnp.where(inside, LATITUDE_RATE, 0.0).astype(jnp.float32)
    for offset in range(LSTEPS):
        height = extended.shape[1]
        north_rate = face_rate[offset + 1 : offset + height - 1][None, :, None]
        south_rate = face_rate[offset : offset + height - 2][None, :, None]
        center = extended[:, 1:-1]
        extended = (
            center
            + north_rate * (extended[:, 2:] - center)
            + south_rate * (extended[:, :-2] - center)
        )
    return extended


def shards(ensemble, gradient, previous, diffusivity):
    band_index = lax.axis_index(BAND)
    tile_rows = gradient.shape[1]
    total_rows = tile_rows * lax.axis_size(BAND)
    padded_rate = padded(diffusivity, ((MEM, 2), (BAND, 1)), 4, True)
    east_faces, north_faces = fine_faces(padded_rate, band_index * tile_rows - 4, total_rows)

    def run_sweep(turn_index, state_field):
        extended = padded(state_field, ((MEM, 2), (BAND, 1)), 4, True)
        for offset in range(4):
            extended = fine_substep(extended, east_faces, north_faces, offset)
        return extended

    smoothed = lax.fori_loop(0, SUBSTEPS // 4, run_sweep, gradient)
    variables = gradient.shape[0]
    coarse_rows = ensemble.shape[2]
    coarse_cols = gradient.shape[2] // REFINE
    total_coarse = coarse_rows * lax.axis_size(BAND)
    restricted = gradient.reshape(variables, coarse_rows, REFINE, coarse_cols, REFINE).sum(
        axis=(2, 4)
    ) * (1.0 / (REFINE * REFINE))
    kernel = longitude_kernel(NLON, LOCLON)
    members_all = ensemble.shape[0] * lax.axis_size(MEM)
    inverse_count = 1.0 / (members_all - 1)
    gathered = gather_directly(restricted, MEM, 2)
    control = jnp.sum(ensemble * gathered[None], axis=1)
    blended = localize(control, kernel, band_index, total_coarse)
    member_terms = jnp.sum(ensemble * blended[:, None], axis=0)
    ensemble_part = sum_at_owner(member_terms, MEM, 2) * inverse_count
    injected = jnp.broadcast_to(
        ensemble_part[:, :, None, :, None], (variables, coarse_rows, REFINE, coarse_cols, REFINE)
    ).reshape(gradient.shape)
    direction = HYBRID_WEIGHT * smoothed + HYBRID_WEIGHT * injected
    along_sum, square_sum = (
        one_axis_at_a_time(jnp.sum(gradient * direction), MEM_BAND),
        one_axis_at_a_time(jnp.sum(direction * direction), MEM_BAND),
    )
    analysis = previous - along_sum / (along_sum + square_sum) * direction
    return (analysis, direction)


def solution(mesh):
    split = Mesh(
        mesh.devices.reshape(2, 8, 4, 8, 2), ("mem_0", "mem_1", "band_0", "band_1", "band_2")
    )
    return jax.shard_map(
        shards,
        mesh=split,
        in_specs=(
            P(MEM, None, BAND, None),
            P(None, BAND, MEM),
            P(None, BAND, MEM),
            P(None, BAND, MEM),
        ),
        out_specs=(P(None, BAND, MEM), P(None, BAND, MEM)),
        check_vma=False,
    )
```

profile of v0, /device:TPU:1, one launch (start us, length us, event | category | flops | bytes accessed | tf_op | source)
XLA Modules:
  0.0 237.5 jit_solution(11376840700773136886)
XLA Ops:
  0.6 3.9 %reshape.38 = f32[4,4,4,90,4]{4,3,2,1,0:T(8,128)S(1)} reshape(f32[4,16,360]{2,1,0:T(8,128)} %param.7) | data formatting | bytes 184320 | tf_op jit(solution)/shard_map/reshape | solution.py:150
  4.6 0.4 reduce_sum.54
  5.0 0.7 broadcast_in_dim.24
  5.6 9.1 %all-to-all-start = ((f32[16,4,4,90]{3,2,1,0:T(4,128)}), f32[16,4,4,90]{3,2,1,0:T(4,128)S(1)}, u32[]{:S(2)}, u32[]{:S(2)}) async-start(f32[16,4,4,90]{3,2,1,0:T(4,128)} %broadcast_in_dim.24), calls=%async_computation | async-start | bytes 262144 | tf_op jit(solution)/shard_map/all_to_all | solution.py:38
  14.8 0.9 fusion.69
  15.6 3.3 %collective-permute-start.4 = (f32[4,16,4]{2,1,0:T(8,128)S(1)}, f32[4,16,4]{2,1,0:T(8,128)S(1)}, u32[]{:S(2)}, u32[]{:S(2)}) collective-permute-start(f32[4,16,4]{2,1,0:T(8,128)S(1)} %get-tuple-element.53), channel_id=1, source_target_pairs={{0,64},{64,128},{128,192},{192,256},{256,320},{320,384},{384,448},... | collective-permute-start | bytes 3080 | tf_op jit(solution)/shard_map/ppermute | solution.py:28
  18.9 4.1 %collective-permute-start.5 = (f32[4,16,4]{2,1,0:T(8,128)S(1)}, f32[4,16,4]{2,1,0:T(8,128)S(1)}, u32[]{:S(2)}, u32[]{:S(2)}) collective-permute-start(f32[4,16,4]{2,1,0:T(8,128)S(1)} %get-tuple-element.54), channel_id=1, source_target_pairs={{64,0},{128,64},{192,128},{256,192},{320,256},{384,320},{448,384},... | collective-permute-start | bytes 3080 | tf_op jit(solution)/shard_map/ppermute | solution.py:31
  23.3 0.7 collective-permute-done.5
  24.0 0.9 pad_maximum_fusion.8
  24.9 7.0 %collective-permute-start.6 = (f32[4,4,368]{2,1,0:T(4,128)S(1)}, f32[4,4,368]{2,1,0:T(4,128)S(1)}, u32[]{:S(2)}, u32[]{:S(2)}) collective-permute-start(f32[4,4,368]{2,1,0:T(4,128)S(1)} %get-tuple-element.51), channel_id=1, source_target_pairs={{0,1},{1,2},{2,3},{3,4},{4,5},{5,6},{6,7},{7,8},{8,9},{9,10},{10,1... | collective-permute-start | bytes 70664 | tf_op jit(solution)/shard_map/ppermute | solution.py:28
  31.9 6.5 %collective-permute-start.7 = (f32[4,4,368]{2,1,0:T(4,128)S(1)}, f32[4,4,368]{2,1,0:T(4,128)S(1)}, u32[]{:S(2)}, u32[]{:S(2)}) collective-permute-start(f32[4,4,368]{2,1,0:T(4,128)S(1)} %get-tuple-element.52), channel_id=1, source_target_pairs={{1,0},{2,1},{3,2},{4,3},{5,4},{6,5},{7,6},{8,7},{9,8},{10,9},{11,1... | collective-permute-start | bytes 70664 | tf_op jit(solution)/shard_map/ppermute | solution.py:31
  38.4 0.8 collective-permute-done.7
  39.2 1.0 pad_maximum_fusion.5
  40.6 7.2 %fusion.37 = f32[4,4,1440]{2,1,0:T(4,128)S(1)} fusion(f32[4,4,1440]{2,1,0:T(4,128)S(1)} %multiply_reduce_fusion.1), kind=kOutput, calls=%fused_computation.58 | convolution fusion | flops 412646400 | bytes 184320 | tf_op jit(solution)/shard_map/dot_general | solution.py:111
  47.8 1.9 collective-permute-start.8
  49.7 10.1 %collective-permute-start.9 = (f32[4,4,1440]{2,1,0:T(4,128)S(1)}, f32[4,4,1440]{2,1,0:T(4,128)S(1)}, u32[]{:S(2)}, u32[]{:S(2)}) collective-permute-start(f32[4,4,1440]{2,1,0:T(4,128)S(1)} %fusion.37), channel_id=1, source_target_pairs={{1,0},{2,1},{3,2},{4,3},{5,4},{6,5},{7,6},{8,7},{9,8},{10,9},{11,1... | collective-permute-start | bytes 276488 | tf_op jit(solution)/shard_map/ppermute | solution.py:31
  59.9 0.8 collective-permute-done.9
  61.6 0.7 copy.7
  62.3 7.2 %all-to-all-start.1 = ((f32[16,4,4,90]{3,2,1,0:T(4,128)}), f32[16,4,4,90]{3,2,1,0:T(4,128)S(1)}, u32[]{:S(2)}, u32[]{:S(2)}) async-start(f32[16,4,4,90]{3,2,1,0:T(4,128)} %copy.7), calls=%async_computation.1 | async-start | bytes 262144 | tf_op jit(solution)/shard_map/all_to_all | solution.py:59
  69.6 7.3 %all-to-all-done.1 = f32[16,4,4,90]{3,2,1,0:T(4,128)S(1)} async-done(((f32[16,4,4,90]{3,2,1,0:T(4,128)}), f32[16,4,4,90]{3,2,1,0:T(4,128)S(1)}, u32[]{:S(2)}, u32[]{:S(2)}) %all-to-all-start.1) | async-done | bytes 92192 | tf_op jit(solution)/shard_map/all_to_all | solution.py:59
  77.0 0.4 broadcast_in_dim.27
  77.4 3.2 %reshape.40 = f32[4,16,360]{2,1,0:T(8,128)} reshape(f32[4,4,4,90,4]{4,3,2,1,0:T(8,128)S(1)} %broadcast_in_dim.27) | data formatting | bytes 184320 | tf_op jit(solution)/shard_map/reshape | solution.py:163
  80.6 92.9 %while.10 = (s32[]{:T(128)}, f32[4,16,360]{2,1,0:T(8,128)S(1)}, f32[4,24,367]{2,1,0:T(8,128)S(1)}, f32[4,23,368]{2,1,0:T(8,128)S(1)}, s32[]{:T(128)}) while((s32[]{:T(128)}, f32[4,16,360]{2,1,0:T(8,128)S(1)}, f32[4,24,367]{2,1,0:T(8,128)S(1)}, f32[4,23,368]{2,1,0:T(8,128)S(1)}, s32[]{:T(128)}) %tuple.40), condition=%wide.region_1.2_spmd, body=%wide.region_0.1_spmd.sunk | while | flops 1490050 | bytes 5042141 | solution.py:145
  80.7 3.6 %collective-permute-start = (f32[4,16,4]{2,1,0:T(8,128)S(1)}, f32[4,16,4]{2,1,0:T(8,128)S(1)}, u32[]{:S(2)}, u32[]{:S(2)}) collective-permute-start(f32[4,16,4]{2,1,0:T(8,128)S(1)} %get-tuple-element.92), channel_id=1, source_target_pairs={{64,0},{128,64},{192,128},{256,192},{320,256},{384,320},{448,384},... | collective-permute-start | bytes 3080 | tf_op jit(solution)/shard_map/while/body/eval_jaxpr/ppermute | solution.py:31
  84.3 1.9 collective-permute-start.1
  86.2 4.8 %collective-permute-done.1 = f32[4,16,4]{2,1,0:T(8,128)S(1)} collective-permute-done((f32[4,16,4]{2,1,0:T(8,128)S(1)}, f32[4,16,4]{2,1,0:T(8,128)S(1)}, u32[]{:S(2)}, u32[]{:S(2)}) %collective-permute-start.1) | collective-permute-done | bytes 1056 | tf_op jit(solution)/shard_map/while/body/eval_jaxpr/ppermute | solution.py:28
  91.1 5.4 %collective-permute-start.2 = (f32[4,4,368]{2,1,0:T(4,128)S(1)}, f32[4,4,368]{2,1,0:T(4,128)S(1)}, u32[]{:S(2)}, u32[]{:S(2)}) collective-permute-start(f32[4,4,368]{2,1,0:T(4,128)S(1)} %get-tuple-element.94), channel_id=1, source_target_pairs={{1,0},{2,1},{3,2},{4,3},{5,4},{6,5},{7,6},{8,7},{9,8},{10,9},{11,1... | collective-permute-start | bytes 70664 | tf_op jit(solution)/shard_map/while/body/eval_jaxpr/ppermute | solution.py:31
  96.5 1.9 collective-permute-start.3
  98.5 4.5 %collective-permute-done.3 = f32[4,4,368]{2,1,0:T(4,128)S(1)} collective-permute-done((f32[4,4,368]{2,1,0:T(4,128)S(1)}, f32[4,4,368]{2,1,0:T(4,128)S(1)}, u32[]{:S(2)}, u32[]{:S(2)}) %collective-permute-start.3) | collective-permute-done | bytes 23584 | tf_op jit(solution)/shard_map/while/body/eval_jaxpr/ppermute | solution.py:28
  103.1 0.3 fusion.81
  103.4 0.4 fusion.82
  103.8 0.4 fusion.83
  104.6 1.9 collective-permute-start
  106.5 3.4 %collective-permute-start.1 = (f32[4,16,4]{2,1,0:T(8,128)S(1)}, f32[4,16,4]{2,1,0:T(8,128)S(1)}, u32[]{:S(2)}, u32[]{:S(2)}) collective-permute-start(f32[4,16,4]{2,1,0:T(8,128)S(1)} %get-tuple-element.93), channel_id=1, source_target_pairs={{0,64},{64,128},{128,192},{192,256},{256,320},{320,384},{384,448},... | collective-permute-start | bytes 3080 | tf_op jit(solution)/shard_map/while/body/eval_jaxpr/ppermute | solution.py:28
  109.9 3.4 %collective-permute-done.1 = f32[4,16,4]{2,1,0:T(8,128)S(1)} collective-permute-done((f32[4,16,4]{2,1,0:T(8,128)S(1)}, f32[4,16,4]{2,1,0:T(8,128)S(1)}, u32[]{:S(2)}, u32[]{:S(2)}) %collective-permute-start.1) | collective-permute-done | bytes 1056 | tf_op jit(solution)/shard_map/while/body/eval_jaxpr/ppermute | solution.py:28
  113.4 9.8 %collective-permute-start.2 = (f32[4,4,368]{2,1,0:T(4,128)S(1)}, f32[4,4,368]{2,1,0:T(4,128)S(1)}, u32[]{:S(2)}, u32[]{:S(2)}) collective-permute-start(f32[4,4,368]{2,1,0:T(4,128)S(1)} %get-tuple-element.94), channel_id=1, source_target_pairs={{1,0},{2,1},{3,2},{4,3},{5,4},{6,5},{7,6},{8,7},{9,8},{10,9},{11,1... | collective-permute-start | bytes 70664 | tf_op jit(solution)/shard_map/while/body/eval_jaxpr/ppermute | solution.py:31
  123.2 1.9 collective-permute-start.3
  125.1 1.2 collective-permute-done.3
  126.4 0.3 fusion.81
  126.8 0.4 fusion.82
  127.2 0.4 fusion.83
  127.9 1.9 collective-permute-start
  129.8 3.4 %collective-permute-start.1 = (f32[4,16,4]{2,1,0:T(8,128)S(1)}, f32[4,16,4]{2,1,0:T(8,128)S(1)}, u32[]{:S(2)}, u32[]{:S(2)}) collective-permute-start(f32[4,16,4]{2,1,0:T(8,128)S(1)} %get-tuple-element.93), channel_id=1, source_target_pairs={{0,64},{64,128},{128,192},{192,256},{256,320},{320,384},{384,448},... | collective-permute-start | bytes 3080 | tf_op jit(solution)/shard_map/while/body/eval_jaxpr/ppermute | solution.py:28
  133.2 3.4 %collective-permute-done.1 = f32[4,16,4]{2,1,0:T(8,128)S(1)} collective-permute-done((f32[4,16,4]{2,1,0:T(8,128)S(1)}, f32[4,16,4]{2,1,0:T(8,128)S(1)}, u32[]{:S(2)}, u32[]{:S(2)}) %collective-permute-start.1) | collective-permute-done | bytes 1056 | tf_op jit(solution)/shard_map/while/body/eval_jaxpr/ppermute | solution.py:28
  136.7 9.3 %collective-permute-start.2 = (f32[4,4,368]{2,1,0:T(4,128)S(1)}, f32[4,4,368]{2,1,0:T(4,128)S(1)}, u32[]{:S(2)}, u32[]{:S(2)}) collective-permute-start(f32[4,4,368]{2,1,0:T(4,128)S(1)} %get-tuple-element.94), channel_id=1, source_target_pairs={{1,0},{2,1},{3,2},{4,3},{5,4},{6,5},{7,6},{8,7},{9,8},{10,9},{11,1... | collective-permute-start | bytes 70664 | tf_op jit(solution)/shard_map/while/body/eval_jaxpr/ppermute | solution.py:31
  146.1 1.9 collective-permute-start.3
  148.0 1.2 collective-permute-done.3
  149.6 0.4 fusion.82
  150.0 0.4 fusion.83
  150.8 1.9 collective-permute-start
  152.7 3.4 %collective-permute-start.1 = (f32[4,16,4]{2,1,0:T(8,128)S(1)}, f32[4,16,4]{2,1,0:T(8,128)S(1)}, u32[]{:S(2)}, u32[]{:S(2)}) collective-permute-start(f32[4,16,4]{2,1,0:T(8,128)S(1)} %get-tuple-element.93), channel_id=1, source_target_pairs={{0,64},{64,128},{128,192},{192,256},{256,320},{320,384},{384,448},... | collective-permute-start | bytes 3080 | tf_op jit(solution)/shard_map/while/body/eval_jaxpr/ppermute | solution.py:28
  156.1 3.4 %collective-permute-done.1 = f32[4,16,4]{2,1,0:T(8,128)S(1)} collective-permute-done((f32[4,16,4]{2,1,0:T(8,128)S(1)}, f32[4,16,4]{2,1,0:T(8,128)S(1)}, u32[]{:S(2)}, u32[]{:S(2)}) %collective-permute-start.1) | collective-permute-done | bytes 1056 | tf_op jit(solution)/shard_map/while/body/eval_jaxpr/ppermute | solution.py:28
  159.6 9.3 %collective-permute-start.2 = (f32[4,4,368]{2,1,0:T(4,128)S(1)}, f32[4,4,368]{2,1,0:T(4,128)S(1)}, u32[]{:S(2)}, u32[]{:S(2)}) collective-permute-start(f32[4,4,368]{2,1,0:T(4,128)S(1)} %get-tuple-element.94), channel_id=1, source_target_pairs={{1,0},{2,1},{3,2},{4,3},{5,4},{6,5},{7,6},{8,7},{9,8},{10,9},{11,1... | collective-permute-start | bytes 70664 | tf_op jit(solution)/shard_map/while/body/eval_jaxpr/ppermute | solution.py:31
  168.9 1.9 collective-permute-start.3
  170.8 1.2 collective-permute-done.3
  172.5 0.4 fusion.82
  172.9 0.4 fusion.83
  173.5 1.3 multiply_reduce_fusion.2
  174.9 4.4 %all-reduce.4 = (f32[]{:T(128)}, f32[]{:T(128)}) all-reduce(f32[]{:T(128)} %get-tuple-element.26, f32[]{:T(128)} %get-tuple-element.25), channel_id=1, replica_groups=mesh['mem_0'=2,'mem_1'=8,'band_0'=4,'band_1'=8,'band_2'=2] {'mem_0'}, use_global_device_ids=true, to_apply=%region_7.8 | all-reduce | flops 2 | bytes 16 | tf_op jit(solution)/shard_map/psum | solution.py:65
  179.3 11.4 %all-reduce.1 = (f32[]{:T(128)}, f32[]{:T(128)}) all-reduce(f32[]{:T(128)} %get-tuple-element.43, f32[]{:T(128)} %get-tuple-element.44), channel_id=1, replica_groups=mesh['mem_0'=2,'mem_1'=8,'band_0'=4,'band_1'=8,'band_2'=2] {'mem_1'}, use_global_device_ids=true, to_apply=%region_8.9 | all-reduce | flops 2 | bytes 16 | tf_op jit(solution)/shard_map/psum | solution.py:65
  190.7 14.0 %all-reduce.2 = (f32[]{:T(128)}, f32[]{:T(128)}) all-reduce(f32[]{:T(128)} %get-tuple-element.37, f32[]{:T(128)} %get-tuple-element.38), channel_id=1, replica_groups=mesh['mem_0'=2,'mem_1'=8,'band_0'=4,'band_1'=8,'band_2'=2] {'band_0'}, use_global_device_ids=true, to_apply=%region_9.10 | all-reduce | flops 2 | bytes 16 | tf_op jit(solution)/shard_map/psum | solution.py:65
  204.7 17.2 %all-reduce = (f32[]{:T(128)}, f32[]{:T(128)}) all-reduce(f32[]{:T(128)} %get-tuple-element.39, f32[]{:T(128)} %get-tuple-element.40), channel_id=1, replica_groups=mesh['mem_0'=2,'mem_1'=8,'band_0'=4,'band_1'=8,'band_2'=2] {'band_1'}, use_global_device_ids=true, to_apply=%region_10.11 | all-reduce | flops 2 | bytes 16 | tf_op jit(solution)/shard_map/psum | solution.py:65
  221.9 13.0 %all-reduce.3 = (f32[]{:T(128)}, f32[]{:T(128)}) all-reduce(f32[]{:T(128)} %get-tuple-element.35, f32[]{:T(128)} %get-tuple-element.36), channel_id=1, replica_groups=mesh['mem_0'=2,'mem_1'=8,'band_0'=4,'band_1'=8,'band_2'=2] {'band_2'}, use_global_device_ids=true, to_apply=%region_11.12 | all-reduce | flops 2 | bytes 16 | tf_op jit(solution)/shard_map/psum | solution.py:65
  236.9 0.7 multiply_subtract_fusion
  (61 shorter events, 4.6 us)
Async XLA Ops:
  4.6 35.9 %copy-start.2 = (f32[4,4,4,1440]{3,2,1,0:T(4,128)S(1)}, f32[4,4,4,1440]{3,2,1,0:T(4,128)}, u32[]{:S(2)}) copy-start(f32[4,4,4,1440]{3,2,1,0:T(4,128)} %param.6) | copy-start | bytes 1105924
  5.6 34.6 %all-to-all-start = ((f32[16,4,4,90]{3,2,1,0:T(4,128)}), f32[16,4,4,90]{3,2,1,0:T(4,128)S(1)}, u32[]{:S(2)}, u32[]{:S(2)}) async-start(f32[16,4,4,90]{3,2,1,0:T(4,128)} %broadcast_in_dim.24), calls=%async_computation | async-start | bytes 262144 | tf_op jit(solution)/shard_map/all_to_all | solution.py:38
  15.6 7.7 %collective-permute-start.4 = (f32[4,16,4]{2,1,0:T(8,128)S(1)}, f32[4,16,4]{2,1,0:T(8,128)S(1)}, u32[]{:S(2)}, u32[]{:S(2)}) collective-permute-start(f32[4,16,4]{2,1,0:T(8,128)S(1)} %get-tuple-element.53), channel_id=1, source_target_pairs={{0,64},{64,128},{128,192},{192,256},{256,320},{320,384},{384,448},... | collective-permute-start | bytes 3080 | tf_op jit(solution)/shard_map/ppermute | solution.py:28
  18.9 5.1 %collective-permute-start.5 = (f32[4,16,4]{2,1,0:T(8,128)S(1)}, f32[4,16,4]{2,1,0:T(8,128)S(1)}, u32[]{:S(2)}, u32[]{:S(2)}) collective-permute-start(f32[4,16,4]{2,1,0:T(8,128)S(1)} %get-tuple-element.54), channel_id=1, source_target_pairs={{64,0},{128,64},{192,128},{256,192},{320,256},{384,320},{448,384},... | collective-permute-start | bytes 3080 | tf_op jit(solution)/shard_map/ppermute | solution.py:31
  24.9 13.5 %collective-permute-start.6 = (f32[4,4,368]{2,1,0:T(4,128)S(1)}, f32[4,4,368]{2,1,0:T(4,128)S(1)}, u32[]{:S(2)}, u32[]{:S(2)}) collective-permute-start(f32[4,4,368]{2,1,0:T(4,128)S(1)} %get-tuple-element.51), channel_id=1, source_target_pairs={{0,1},{1,2},{2,3},{3,4},{4,5},{5,6},{6,7},{7,8},{8,9},{9,10},{10,1... | collective-permute-start | bytes 70664 | tf_op jit(solution)/shard_map/ppermute | solution.py:28
  31.9 7.3 %collective-permute-start.7 = (f32[4,4,368]{2,1,0:T(4,128)S(1)}, f32[4,4,368]{2,1,0:T(4,128)S(1)}, u32[]{:S(2)}, u32[]{:S(2)}) collective-permute-start(f32[4,4,368]{2,1,0:T(4,128)S(1)} %get-tuple-element.52), channel_id=1, source_target_pairs={{1,0},{2,1},{3,2},{4,3},{5,4},{6,5},{7,6},{8,7},{9,8},{10,9},{11,1... | collective-permute-start | bytes 70664 | tf_op jit(solution)/shard_map/ppermute | solution.py:31
  47.8 12.1 %collective-permute-start.8 = (f32[4,4,1440]{2,1,0:T(4,128)S(1)}, f32[4,4,1440]{2,1,0:T(4,128)S(1)}, u32[]{:S(2)}, u32[]{:S(2)}) collective-permute-start(f32[4,4,1440]{2,1,0:T(4,128)S(1)} %fusion.37), channel_id=1, source_target_pairs={{0,1},{1,2},{2,3},{3,4},{4,5},{5,6},{6,7},{7,8},{8,9},{9,10},{10,1... | collective-permute-start | bytes 276488 | tf_op jit(solution)/shard_map/ppermute | solution.py:28
  49.7 11.1 %collective-permute-start.9 = (f32[4,4,1440]{2,1,0:T(4,128)S(1)}, f32[4,4,1440]{2,1,0:T(4,128)S(1)}, u32[]{:S(2)}, u32[]{:S(2)}) collective-permute-start(f32[4,4,1440]{2,1,0:T(4,128)S(1)} %fusion.37), channel_id=1, source_target_pairs={{1,0},{2,1},{3,2},{4,3},{5,4},{6,5},{7,6},{8,7},{9,8},{10,9},{11,1... | collective-permute-start | bytes 276488 | tf_op jit(solution)/shard_map/ppermute | solution.py:31
  62.3 14.7 %all-to-all-start.1 = ((f32[16,4,4,90]{3,2,1,0:T(4,128)}), f32[16,4,4,90]{3,2,1,0:T(4,128)S(1)}, u32[]{:S(2)}, u32[]{:S(2)}) async-start(f32[16,4,4,90]{3,2,1,0:T(4,128)} %copy.7), calls=%async_computation.1 | async-start | bytes 262144 | tf_op jit(solution)/shard_map/all_to_all | solution.py:59
  77.0 3.6 %copy-start.1 = (f32[4,16,360]{2,1,0:T(8,128)S(1)}, f32[4,16,360]{2,1,0:T(8,128)}, u32[]{:S(2)}) copy-start(f32[4,16,360]{2,1,0:T(8,128)} %param.7) | copy-start | bytes 276484
  80.6 93.0 %copy-start = (f32[4,16,360]{2,1,0:T(8,128)S(1)}, f32[4,16,360]{2,1,0:T(8,128)}, u32[]{:S(2)}) copy-start(f32[4,16,360]{2,1,0:T(8,128)} %param.7) | copy-start | bytes 276484
  80.6 93.0 %copy-start.3 = (f32[4,16,360]{2,1,0:T(8,128)S(1)}, f32[4,16,360]{2,1,0:T(8,128)}, u32[]{:S(2)}) copy-start(f32[4,16,360]{2,1,0:T(8,128)} %reshape.40) | copy-start | bytes 276484
  80.6 156.3 %copy-start.4 = (f32[4,16,360]{2,1,0:T(8,128)S(1)}, f32[4,16,360]{2,1,0:T(8,128)}, u32[]{:S(2)}) copy-start(f32[4,16,360]{2,1,0:T(8,128)} %param.8) | copy-start | bytes 276484
  80.7 5.5 %collective-permute-start = (f32[4,16,4]{2,1,0:T(8,128)S(1)}, f32[4,16,4]{2,1,0:T(8,128)S(1)}, u32[]{:S(2)}, u32[]{:S(2)}) collective-permute-start(f32[4,16,4]{2,1,0:T(8,128)S(1)} %get-tuple-element.92), channel_id=1, source_target_pairs={{64,0},{128,64},{192,128},{256,192},{320,256},{384,320},{448,384},... | collective-permute-start | bytes 3080 | tf_op jit(solution)/shard_map/while/body/eval_jaxpr/ppermute | solution.py:31
  84.3 6.8 %collective-permute-start.1 = (f32[4,16,4]{2,1,0:T(8,128)S(1)}, f32[4,16,4]{2,1,0:T(8,128)S(1)}, u32[]{:S(2)}, u32[]{:S(2)}) collective-permute-start(f32[4,16,4]{2,1,0:T(8,128)S(1)} %get-tuple-element.93), channel_id=1, source_target_pairs={{0,64},{64,128},{128,192},{192,256},{256,320},{320,384},{384,448},... | collective-permute-start | bytes 3080 | tf_op jit(solution)/shard_map/while/body/eval_jaxpr/ppermute | solution.py:28
  91.1 7.3 %collective-permute-start.2 = (f32[4,4,368]{2,1,0:T(4,128)S(1)}, f32[4,4,368]{2,1,0:T(4,128)S(1)}, u32[]{:S(2)}, u32[]{:S(2)}) collective-permute-start(f32[4,4,368]{2,1,0:T(4,128)S(1)} %get-tuple-element.94), channel_id=1, source_target_pairs={{1,0},{2,1},{3,2},{4,3},{5,4},{6,5},{7,6},{8,7},{9,8},{10,9},{11,1... | collective-permute-start | bytes 70664 | tf_op jit(solution)/shard_map/while/body/eval_jaxpr/ppermute | solution.py:31
  96.5 6.4 %collective-permute-start.3 = (f32[4,4,368]{2,1,0:T(4,128)S(1)}, f32[4,4,368]{2,1,0:T(4,128)S(1)}, u32[]{:S(2)}, u32[]{:S(2)}) collective-permute-start(f32[4,4,368]{2,1,0:T(4,128)S(1)} %get-tuple-element.95), channel_id=1, source_target_pairs={{0,1},{1,2},{2,3},{3,4},{4,5},{5,6},{6,7},{7,8},{8,9},{9,10},{10,1... | collective-permute-start | bytes 70664 | tf_op jit(solution)/shard_map/while/body/eval_jaxpr/ppermute | solution.py:28
  104.6 5.3 %collective-permute-start = (f32[4,16,4]{2,1,0:T(8,128)S(1)}, f32[4,16,4]{2,1,0:T(8,128)S(1)}, u32[]{:S(2)}, u32[]{:S(2)}) collective-permute-start(f32[4,16,4]{2,1,0:T(8,128)S(1)} %get-tuple-element.92), channel_id=1, source_target_pairs={{64,0},{128,64},{192,128},{256,192},{320,256},{384,320},{448,384},... | collective-permute-start | bytes 3080 | tf_op jit(solution)/shard_map/while/body/eval_jaxpr/ppermute | solution.py:31
  106.5 6.8 %collective-permute-start.1 = (f32[4,16,4]{2,1,0:T(8,128)S(1)}, f32[4,16,4]{2,1,0:T(8,128)S(1)}, u32[]{:S(2)}, u32[]{:S(2)}) collective-permute-start(f32[4,16,4]{2,1,0:T(8,128)S(1)} %get-tuple-element.93), channel_id=1, source_target_pairs={{0,64},{64,128},{128,192},{192,256},{256,320},{320,384},{384,448},... | collective-permute-start | bytes 3080 | tf_op jit(solution)/shard_map/while/body/eval_jaxpr/ppermute | solution.py:28
  113.4 11.8 %collective-permute-start.2 = (f32[4,4,368]{2,1,0:T(4,128)S(1)}, f32[4,4,368]{2,1,0:T(4,128)S(1)}, u32[]{:S(2)}, u32[]{:S(2)}) collective-permute-start(f32[4,4,368]{2,1,0:T(4,128)S(1)} %get-tuple-element.94), channel_id=1, source_target_pairs={{1,0},{2,1},{3,2},{4,3},{5,4},{6,5},{7,6},{8,7},{9,8},{10,9},{11,1... | collective-permute-start | bytes 70664 | tf_op jit(solution)/shard_map/while/body/eval_jaxpr/ppermute | solution.py:31
  123.2 3.1 %collective-permute-start.3 = (f32[4,4,368]{2,1,0:T(4,128)S(1)}, f32[4,4,368]{2,1,0:T(4,128)S(1)}, u32[]{:S(2)}, u32[]{:S(2)}) collective-permute-start(f32[4,4,368]{2,1,0:T(4,128)S(1)} %get-tuple-element.95), channel_id=1, source_target_pairs={{0,1},{1,2},{2,3},{3,4},{4,5},{5,6},{6,7},{7,8},{8,9},{9,10},{10,1... | collective-permute-start | bytes 70664 | tf_op jit(solution)/shard_map/while/body/eval_jaxpr/ppermute | solution.py:28
  127.9 5.3 %collective-permute-start = (f32[4,16,4]{2,1,0:T(8,128)S(1)}, f32[4,16,4]{2,1,0:T(8,128)S(1)}, u32[]{:S(2)}, u32[]{:S(2)}) collective-permute-start(f32[4,16,4]{2,1,0:T(8,128)S(1)} %get-tuple-element.92), channel_id=1, source_target_pairs={{64,0},{128,64},{192,128},{256,192},{320,256},{384,320},{448,384},... | collective-permute-start | bytes 3080 | tf_op jit(solution)/shard_map/while/body/eval_jaxpr/ppermute | solution.py:31
  129.8 6.8 %collective-permute-start.1 = (f32[4,16,4]{2,1,0:T(8,128)S(1)}, f32[4,16,4]{2,1,0:T(8,128)S(1)}, u32[]{:S(2)}, u32[]{:S(2)}) collective-permute-start(f32[4,16,4]{2,1,0:T(8,128)S(1)} %get-tuple-element.93), channel_id=1, source_target_pairs={{0,64},{64,128},{128,192},{192,256},{256,320},{320,384},{384,448},... | collective-permute-start | bytes 3080 | tf_op jit(solution)/shard_map/while/body/eval_jaxpr/ppermute | solution.py:28
  136.7 11.3 %collective-permute-start.2 = (f32[4,4,368]{2,1,0:T(4,128)S(1)}, f32[4,4,368]{2,1,0:T(4,128)S(1)}, u32[]{:S(2)}, u32[]{:S(2)}) collective-permute-start(f32[4,4,368]{2,1,0:T(4,128)S(1)} %get-tuple-element.94), channel_id=1, source_target_pairs={{1,0},{2,1},{3,2},{4,3},{5,4},{6,5},{7,6},{8,7},{9,8},{10,9},{11,1... | collective-permute-start | bytes 70664 | tf_op jit(solution)/shard_map/while/body/eval_jaxpr/ppermute | solution.py:31
  146.1 3.1 %collective-permute-start.3 = (f32[4,4,368]{2,1,0:T(4,128)S(1)}, f32[4,4,368]{2,1,0:T(4,128)S(1)}, u32[]{:S(2)}, u32[]{:S(2)}) collective-permute-start(f32[4,4,368]{2,1,0:T(4,128)S(1)} %get-tuple-element.95), channel_id=1, source_target_pairs={{0,1},{1,2},{2,3},{3,4},{4,5},{5,6},{6,7},{7,8},{8,9},{9,10},{10,1... | collective-permute-start | bytes 70664 | tf_op jit(solution)/shard_map/while/body/eval_jaxpr/ppermute | solution.py:28
  150.8 5.3 %collective-permute-start = (f32[4,16,4]{2,1,0:T(8,128)S(1)}, f32[4,16,4]{2,1,0:T(8,128)S(1)}, u32[]{:S(2)}, u32[]{:S(2)}) collective-permute-start(f32[4,16,4]{2,1,0:T(8,128)S(1)} %get-tuple-element.92), channel_id=1, source_target_pairs={{64,0},{128,64},{192,128},{256,192},{320,256},{384,320},{448,384},... | collective-permute-start | bytes 3080 | tf_op jit(solution)/shard_map/while/body/eval_jaxpr/ppermute | solution.py:31
  152.7 6.8 %collective-permute-start.1 = (f32[4,16,4]{2,1,0:T(8,128)S(1)}, f32[4,16,4]{2,1,0:T(8,128)S(1)}, u32[]{:S(2)}, u32[]{:S(2)}) collective-permute-start(f32[4,16,4]{2,1,0:T(8,128)S(1)} %get-tuple-element.93), channel_id=1, source_target_pairs={{0,64},{64,128},{128,192},{192,256},{256,320},{320,384},{384,448},... | collective-permute-start | bytes 3080 | tf_op jit(solution)/shard_map/while/body/eval_jaxpr/ppermute | solution.py:28
  159.6 11.3 %collective-permute-start.2 = (f32[4,4,368]{2,1,0:T(4,128)S(1)}, f32[4,4,368]{2,1,0:T(4,128)S(1)}, u32[]{:S(2)}, u32[]{:S(2)}) collective-permute-start(f32[4,4,368]{2,1,0:T(4,128)S(1)} %get-tuple-element.94), channel_id=1, source_target_pairs={{1,0},{2,1},{3,2},{4,3},{5,4},{6,5},{7,6},{8,7},{9,8},{10,9},{11,1... | collective-permute-start | bytes 70664 | tf_op jit(solution)/shard_map/while/body/eval_jaxpr/ppermute | solution.py:31
  168.9 3.1 %collective-permute-start.3 = (f32[4,4,368]{2,1,0:T(4,128)S(1)}, f32[4,4,368]{2,1,0:T(4,128)S(1)}, u32[]{:S(2)}, u32[]{:S(2)}) collective-permute-start(f32[4,4,368]{2,1,0:T(4,128)S(1)} %get-tuple-element.95), channel_id=1, source_target_pairs={{0,1},{1,2},{2,3},{3,4},{4,5},{5,6},{6,7},{7,8},{8,9},{9,10},{10,1... | collective-permute-start | bytes 70664 | tf_op jit(solution)/shard_map/while/body/eval_jaxpr/ppermute | solution.py:28
where the time goes:
time: 239 us; the launch traced here: 238 us
  starting transfers between devices  112 us (47%)
  blocking collectives  60.1 us (25%)
  waiting for transfers between devices  32.6 us (14%)
  other arithmetic  11.6 us (5%)
  local copies, waits for them, and re-layouts  10.7 us (4%)
  matrix products  7.23 us (3%)
  between operations  2.83 us (1%)
    ppermute x11, starting transfers between devices, padded(): lax.ppermute(lax.slice_in_dim(block, 0, width, axis=dim), axis, backward)  63.9 us
    psum x5, blocking collectives, one_axis_at_a_time(): shard = lax.psum(shard, axis)  60.1 us
    ppermute x11, starting transfers between devices, padded(): lax.ppermute(lax.slice_in_dim(block, block.shape[dim] - width, None, axis...  31.9 us
    ppermute x11, waiting for transfers between devices, padded(): lax.ppermute(lax.slice_in_dim(block, block.shape[dim] - width, None, axis...  22.9 us
    all_to_all x1, starting transfers between devices, from_everyone(): return lax.all_to_all(copies, axis, split_axis=0, concat_axis=0, tiled=True)  9.13 us
    all_to_all x1, waiting for transfers between devices, sum_at_owner(): lax.all_to_all(blocks, axis, split_axis=0, concat_axis=0, tiled=True)  7.3 us
    dot_general x1, matrix products, localize(): jnp.dot(control.reshape(members * coarse_rows, columns), kernel, precisio...  7.23 us
    all_to_all x1, starting transfers between devices, sum_at_owner(): lax.all_to_all(blocks, axis, split_axis=0, concat_axis=0, tiled=True)  7.22 us
  transfers between devices with their start and end apart: 24, of which 12 were waited for; matrix products, arithmetic and copies ran while one was open for 1% of the time, Pallas kernels for 0%

commit v1 on v0

v1 whole, which is shorter than its diff:
```python
import jax
import jax.numpy as jnp
from jax import lax
from jax.experimental import pallas as pl
from jax.experimental.pallas import tpu as pltpu
from jax.sharding import Mesh
from jax.sharding import PartitionSpec as P

NLON = 1440
REFINE = 4
SUBSTEPS = 16
LSTEPS = 4
LOCLON = 48
BAND = ("band_0", "band_1", "band_2")
MEM = ("mem_0", "mem_1")
ALL = ("mem_0", "mem_1", "band_0", "band_1", "band_2")

LATITUDE_RATE = 0.25
HYBRID_WEIGHT = 0.5
BLOCK = 240
VMEM_LIMIT = 24 << 20


def shifted(block, axis, step):
    count = lax.axis_size(axis)
    return lax.ppermute(block, axis, [(i, (i + step) % count) for i in range(count)])


def everywhere(shard, axis):
    copies = jnp.broadcast_to(shard[None], (lax.axis_size(axis), *shard.shape))
    return lax.all_to_all(copies, axis, split_axis=0, concat_axis=0, tiled=True)


def params():
    return pltpu.CompilerParams(vmem_limit_bytes=VMEM_LIMIT)


def longitude_kernel_body(high_ref, low_ref):
    rows, columns = high_ref.shape
    own = lax.broadcasted_iota(jnp.int32, (rows, columns), 0)
    other = lax.broadcasted_iota(jnp.int32, (rows, columns), 1)
    spacing = jnp.abs(own - other)
    spacing = jnp.minimum(spacing, NLON - spacing).astype(jnp.float32)
    value = jnp.exp(-0.5 * (spacing / LOCLON) ** 2)
    high = value.astype(jnp.bfloat16)
    high_ref[...] = high
    low_ref[...] = (value - high.astype(jnp.float32)).astype(jnp.bfloat16)


def longitude_kernel():
    part = jax.ShapeDtypeStruct((NLON, BLOCK), jnp.bfloat16)
    return pl.pallas_call(
        longitude_kernel_body,
        out_shape=(part, part),
        compiler_params=params(),
        cost_estimate=pl.CostEstimate(
            flops=20 * NLON * BLOCK, transcendentals=NLON * BLOCK, bytes_accessed=4 * NLON * BLOCK
        ),
        name="longitude_kernel",
    )()


def blend_body(ensemble_ref, low_ref, own_ref, high_ref, kernel_high_ref, kernel_low_ref, out_ref, ext_ref):
    members, variables, coarse_rows, columns = ensemble_ref.shape
    ext_rows = coarse_rows + 2 * LSTEPS
    bands = 1
    for axis in BAND:
        bands = bands * lax.axis_size(axis)
    band = lax.axis_index(BAND)
    for m in range(members):
        base = m * ext_rows
        ext_ref[base : base + LSTEPS] = low_ref[m]
        ext_ref[base + LSTEPS : base + LSTEPS + coarse_rows] = own_ref[m]
        ext_ref[base + LSTEPS + coarse_rows : base + ext_rows] = high_ref[m]
    q = ext_ref[...]
    total = members * ext_rows
    place = lax.rem(lax.broadcasted_iota(jnp.int32, (total, 1), 0), ext_rows)
    row = band * coarse_rows - LSTEPS + place
    rows = bands * coarse_rows
    north = jnp.where((row >= 0) & (row < rows - 1), LATITUDE_RATE, 0.0)
    south = jnp.where((row > 0) & (row <= rows - 1), LATITUDE_RATE, 0.0)
    for _ in range(LSTEPS):
        q = (
            q
            + north * (pltpu.roll(q, total - 1, 0) - q)
            + south * (pltpu.roll(q, 1, 0) - q)
        )
    ext_ref[...] = q
    x = jnp.concatenate(
        [
            ext_ref[m * ext_rows + LSTEPS : m * ext_rows + LSTEPS + coarse_rows]
            for m in range(members)
        ],
        axis=0,
    )
    turned = jnp.concatenate(
        [x] + [
            jnp.concatenate([x[:, BLOCK * j :], x[:, : BLOCK * j]], axis=1)
            for j in range(1, NLON // BLOCK)
        ],
        axis=0,
    )
    part = turned.astype(jnp.bfloat16)
    rest = (turned - part.astype(jnp.float32)).astype(jnp.bfloat16)
    kernel_high = kernel_high_ref[...]
    y = jnp.dot(part, kernel_high, preferred_element_type=jnp.float32)
    y = y + jnp.dot(rest, kernel_high, preferred_element_type=jnp.float32)
    y = y + jnp.dot(part, kernel_low_ref[...], preferred_element_type=jnp.float32)
    held = members * coarse_rows
    blended = jnp.concatenate(
        [y[held * j : held * (j + 1)] for j in range(NLON // BLOCK)], axis=1
    )
    for v in range(variables):
        term = ensemble_ref[0, v] * blended[:coarse_rows]
        for m in range(1, members):
            term = term + ensemble_ref[m, v] * blended[m * coarse_rows : (m + 1) * coarse_rows]
        out_ref[v] = term


def blend(ensemble, low, own, high, kernel_high, kernel_low):
    members, variables, coarse_rows, columns = ensemble.shape
    return pl.pallas_call(
        blend_body,
        out_shape=jax.ShapeDtypeStruct((variables, coarse_rows, columns), jnp.float32),
        scratch_shapes=[pltpu.VMEM((members * (coarse_rows + 2 * LSTEPS), columns), jnp.float32)],
        compiler_params=params(),
        cost_estimate=pl.CostEstimate(
            flops=6 * 16 * NLON * NLON, transcendentals=0, bytes_accessed=4 << 20
        ),
        name="blend",
    )(ensemble, low, own, high, kernel_high, kernel_low)


def diffuse_body(low_ref, own_ref, high_ref, out_ref, field_ref, east_ref, north_ref):
    twice, tile_rows, width = own_ref.shape
    variables = twice // 2
    height = 3 * tile_rows
    bands = 1
    for axis in BAND:
        bands = bands * lax.axis_size(axis)
    first = lax.axis_index(BAND) * tile_rows - tile_rows
    row = first + lax.broadcasted_iota(jnp.int32, (height, 1), 0)
    inside = (row >= 0) & (row + 1 <= bands * tile_rows - 1)
    for v in range(variables):
        field_ref[v] = jnp.concatenate([low_ref[v], own_ref[v], high_ref[v]], axis=0)
        w = variables + v
        rate = jnp.concatenate([low_ref[w], own_ref[w], high_ref[w]], axis=0)
        east_ref[v] = jnp.sqrt(rate * pltpu.roll(rate, width - 1, 1))
        north_ref[v] = jnp.where(inside, jnp.sqrt(rate * pltpu.roll(rate, height - 1, 0)), 0.0)

    def substep(_, carry):
        for v in range(variables):
            f = field_ref[v]
            east = east_ref[v] * (pltpu.roll(f, width - 1, 1) - f)
            north = north_ref[v] * (pltpu.roll(f, height - 1, 0) - f)
            change = east - pltpu.roll(east, 1, 1)
            change = change + north - pltpu.roll(north, 1, 0)
            field_ref[v] = f + change
        return carry

    lax.fori_loop(0, SUBSTEPS, substep, 0)
    for v in range(variables):
        out_ref[v] = field_ref[v, tile_rows : 2 * tile_rows, : out_ref.shape[2]]


def diffuse(low, own, high, columns):
    twice, tile_rows, width = own.shape
    variables = twice // 2
    held = pltpu.VMEM((variables, 3 * tile_rows, width), jnp.float32)
    return pl.pallas_call(
        diffuse_body,
        out_shape=jax.ShapeDtypeStruct((variables, tile_rows, columns), jnp.float32),
        scratch_shapes=[held, held, held],
        compiler_params=params(),
        cost_estimate=pl.CostEstimate(
            flops=16 * 12 * variables * 48 * width, transcendentals=0, bytes_accessed=2 << 20
        ),
        name="diffuse",
    )(low, own, high)


def chosen(rows, columns, ratio, by_row):
    own = lax.broadcasted_iota(jnp.int32, (rows, columns), 0)
    other = lax.broadcasted_iota(jnp.int32, (rows, columns), 1)
    same = (other // ratio == own) if by_row else (own // ratio == other)
    return same.astype(jnp.float32)


def shards(ensemble, gradient, previous, diffusivity):
    variables, tile_rows, columns = gradient.shape
    members, _, coarse_rows, _ = ensemble.shape
    coarse_cols = columns // REFINE
    owners = lax.axis_size(MEM)
    row_sums = gradient.reshape(variables * coarse_rows, REFINE, columns).sum(axis=1)
    restricted = jnp.dot(
        row_sums, chosen(columns, coarse_cols, REFINE, False), precision=lax.Precision.HIGHEST
    ) * (1.0 / (REFINE * REFINE))
    gathered = everywhere(restricted.reshape(variables, coarse_rows, coarse_cols), MEM)
    gathered = jnp.moveaxis(gathered, 0, 2).reshape(variables, coarse_rows, NLON)
    both = jnp.concatenate([gradient, diffusivity], axis=0)
    left = shifted(both[:, :, columns - SUBSTEPS :], MEM, 1)
    right = shifted(both[:, :, :SUBSTEPS], MEM, -1)
    spare = -(columns + 2 * SUBSTEPS) % 128
    gap = jnp.zeros((2 * variables, tile_rows, spare), jnp.float32)
    extended = jnp.concatenate([both, right, gap, left], axis=2)
    kernel_high, kernel_low = longitude_kernel()
    control = jnp.sum(ensemble * gathered[None], axis=1)
    control_low = shifted(control, BAND, 1)
    control_high = shifted(control, BAND, -1)
    rows_low = shifted(extended, BAND, 1)
    rows_high = shifted(extended, BAND, -1)
    member_terms = blend(ensemble, control_low, control, control_high, kernel_high, kernel_low)
    blocks = jnp.moveaxis(member_terms.reshape(variables, coarse_rows, owners, coarse_cols), 2, 0)
    arrived = lax.all_to_all(blocks, MEM, split_axis=0, concat_axis=0, tiled=True)
    smoothed = diffuse(rows_low, extended, rows_high, columns)
    inverse_count = 1.0 / (members * owners - 1)
    ensemble_part = arrived.sum(axis=0) * inverse_count
    spread = jnp.dot(
        ensemble_part.reshape(variables * coarse_rows, coarse_cols),
        chosen(coarse_cols, columns, REFINE, True),
        precision=lax.Precision.HIGHEST,
    )
    injected = jnp.broadcast_to(
        spread.reshape(variables, coarse_rows, 1, columns),
        (variables, coarse_rows, REFINE, columns),
    ).reshape(gradient.shape)
    direction = HYBRID_WEIGHT * smoothed + HYBRID_WEIGHT * injected
    along_sum, square_sum = lax.psum(
        (jnp.sum(gradient * direction), jnp.sum(direction * direction)), ALL
    )
    analysis = previous - along_sum / (along_sum + square_sum) * direction
    return (analysis, direction)


def solution(mesh):
    split = Mesh(
        mesh.devices.reshape(2, 8, 4, 8, 2), ("mem_0", "mem_1", "band_0", "band_1", "band_2")
    )
    return jax.shard_map(
        shards,
        mesh=split,
        in_specs=(
            P(MEM, None, BAND, None),
            P(None, BAND, MEM),
            P(None, BAND, MEM),
            P(None, BAND, MEM),
        ),
        out_specs=(P(None, BAND, MEM), P(None, BAND, MEM)),
        check_vma=False,
    )
```

time: 239 us -> 185 us (0.77)
  starting transfers between devices: 112 us -> 47.7 us
  blocking collectives: 60.1 us -> 118 us
  waiting for transfers between devices: 32.6 us -> 0.99 us
  other arithmetic: 11.6 us -> 2.27 us
  Pallas kernels: 0 us -> 8.17 us
  local copies, waits for them, and re-layouts: 10.7 us -> 3.71 us
  matrix products: 7.23 us -> 0.53 us
    ppermute x22 -> x6, starting transfers between devices: 95.8 us -> 32.9 us  [shifted(): lax.ppermute(block, axis, [(i, (i + step) % count) for i in range(count)])]
    psum x5 -> x1, blocking collectives: 60.1 us -> 118 us  [shards(): lax.psum((jnp.sum(gradient * direction), jnp.sum(direction * direction)),...]
    ppermute x22 -> x6, waiting for transfers between devices: 25.3 us -> 0.02 us  [shifted(): lax.ppermute(block, axis, [(i, (i + step) % count) for i in range(count)])]
    pallas_call x0 -> x3, Pallas kernels: none -> 8.17 us  [the longest x1 6.5 us: diffuse(): pl.pallas_call(diffuse_body, out_shape=jax.ShapeDtypeStruct((variables, t...]
    dot_general x1 -> x2, matrix products: 7.23 us -> 0.53 us  [the longest x1 0.35 us: shards(): jnp.dot(row_sums, chosen(columns, coarse_cols, REFINE, False), precision=...]
    all_to_all x2, waiting for transfers between devices: 7.3 us -> 0.98 us  [the longest x1 0.97 us: shards(): lax.all_to_all(blocks, MEM, split_axis=0, concat_axis=0, tiled=True)]
    add x20 -> x0, other arithmetic: 6.01 us -> none  [the longest x16 5.55 us: fine_substep(): return center + change]
    reshape x3 -> x4, local copies, waits for them, and re-layouts: 7.26 us -> 1.8 us  [the longest x1 0.92 us: shards(): gradient.reshape(variables * coarse_rows, REFINE, columns).sum(axis=1)]
  transfers between devices with their start and end apart: 24 -> 8, of which waited for: 12 -> 1; matrix products, arithmetic and copies ran while one was open for 1% -> 1% of each run, Pallas kernels for 0% -> 4%
where the time goes in v1:
time: 185 us; the launch traced here: 184 us
  blocking collectives  118 us (64%)
  starting transfers between devices  47.7 us (26%)
  Pallas kernels  8.17 us (4%)
  local copies, waits for them, and re-layouts  3.71 us (2%)
  between operations  2.83 us (2%)
  other arithmetic  2.27 us (1%)
    psum x1, blocking collectives, shards(): lax.psum((jnp.sum(gradient * direction), jnp.sum(direction * direction)),...  118 us
    ppermute x6, starting transfers between devices, shifted(): lax.ppermute(block, axis, [(i, (i + step) % count) for i in range(count)])  32.9 us
    all_to_all x1, starting transfers between devices, everywhere(): return lax.all_to_all(copies, axis, split_axis=0, concat_axis=0, tiled=True)  9.26 us
    pallas_call x1, Pallas kernels, diffuse(): pl.pallas_call(diffuse_body, out_shape=jax.ShapeDtypeStruct((variables, t...  6.5 us
    all_to_all x1, starting transfers between devices, shards(): lax.all_to_all(blocks, MEM, split_axis=0, concat_axis=0, tiled=True)  5.53 us
  transfers between devices with their start and end apart: 8, of which 1 were waited for; matrix products, arithmetic and copies ran while one was open for 1% of the time, Pallas kernels for 4%

profile of v1, /device:TPU:1, one launch (start us, length us, event | category | flops | bytes accessed | tf_op | source)
XLA Modules:
  0.0 184.4 jit_solution(10245238016689254919)
XLA Ops:
  0.7 0.9 reshape.24
  1.6 0.1 reduce_sum.45
  1.6 0.4 convolution_multiply_fusion
  2.0 0.7 broadcast_in_dim.17
  2.7 0.0 copy-start.1
  2.7 9.3 %all-to-all-start = ((f32[16,4,4,90]{3,2,1,0:T(4,128)}), f32[16,4,4,90]{3,2,1,0:T(4,128)S(1)}, u32[]{:S(2)}, u32[]{:S(2)}) async-start(f32[16,4,4,90]{3,2,1,0:T(4,128)} %broadcast_in_dim.17), calls=%async_computation | async-start | bytes 262144 | tf_op jit(solution)/shard_map/all_to_all | solution.py:31
  11.9 0.0 copy-done.1
  11.9 0.0 copy-start.2
  12.0 0.9 copy-done.2
  12.9 0.0 copy-start
  12.9 0.1 fusion.15
  12.9 5.5 %collective-permute-start = (f32[8,16,16]{2,1,0:T(8,128)S(1)}, f32[8,16,16]{2,1,0:T(8,128)S(1)}, u32[]{:S(2)}, u32[]{:S(2)}) collective-permute-start(f32[8,16,16]{2,1,0:T(8,128)S(1)} %get-tuple-element.12), channel_id=1, source_target_pairs={{0,960},{64,0},{128,64},{192,128},{256,192},{320,256},{384,320},{4... | collective-permute-start | bytes 24584 | tf_op jit(solution)/shard_map/ppermute | solution.py:26
  18.5 1.9 %collective-permute-start.1 = (f32[8,16,16]{2,1,0:T(8,128)S(1)}, f32[8,16,16]{2,1,0:T(8,128)S(1)}, u32[]{:S(2)}, u32[]{:S(2)}) collective-permute-start(f32[8,16,16]{2,1,0:T(8,128)S(1)} %get-tuple-element.13), channel_id=1, source_target_pairs={{0,64},{64,128},{128,192},{192,256},{256,320},{320,384},{384,448},... | collective-permute-start | bytes 24584 | tf_op jit(solution)/shard_map/ppermute | solution.py:26
  20.4 0.1 pad.2.clone
  20.5 0.0 all-to-all-done
  20.5 0.1 mul.44
  20.7 0.0 copy-done
  20.7 0.1 multiply_reduce_fusion.own_ref
  20.8 6.3 %collective-permute-start.4 = (f32[4,4,1440]{2,1,0:T(4,128)S(1)}, f32[4,4,1440]{2,1,0:T(4,128)S(1)}, u32[]{:S(2)}, u32[]{:S(2)}) collective-permute-start(f32[4,4,1440]{2,1,0:T(4,128)S(1)} %multiply_reduce_fusion.own_ref), channel_id=1, source_target_pairs={{0,1},{1,2},{2,3},{3,4},{4,5},{5,6},{6,7},{7,8},{8,9},{9,10},{10,1... | collective-permute-start | bytes 276488 | tf_op jit(solution)/shard_map/ppermute | solution.py:26
  27.1 6.5 %collective-permute-start.5 = (f32[4,4,1440]{2,1,0:T(4,128)S(1)}, f32[4,4,1440]{2,1,0:T(4,128)S(1)}, u32[]{:S(2)}, u32[]{:S(2)}) collective-permute-start(f32[4,4,1440]{2,1,0:T(4,128)S(1)} %multiply_reduce_fusion.own_ref), channel_id=1, source_target_pairs={{0,63},{1,0},{2,1},{3,2},{4,3},{5,4},{6,5},{7,6},{8,7},{9,8},{10,9... | collective-permute-start | bytes 276488 | tf_op jit(solution)/shard_map/ppermute | solution.py:26
  33.6 0.0 collective-permute-done
  33.7 0.0 collective-permute-done.1
  33.7 0.1 pad_maximum_fusion.own_ref
  33.8 1.9 %collective-permute-start.2 = (f32[8,16,512]{2,1,0:T(8,128)S(1)}, f32[8,16,512]{2,1,0:T(8,128)S(1)}, u32[]{:S(2)}, u32[]{:S(2)}) collective-permute-start(f32[8,16,512]{2,1,0:T(8,128)S(1)} %pad_maximum_fusion.own_ref), channel_id=1, source_target_pairs={{0,1},{1,2},{2,3},{3,4},{4,5},{5,6},{6,7},{7,8},{8,9},{9,10},{10,1... | collective-permute-start | bytes 786440 | tf_op jit(solution)/shard_map/ppermute | solution.py:26
  35.7 10.7 %collective-permute-start.3 = (f32[8,16,512]{2,1,0:T(8,128)S(1)}, f32[8,16,512]{2,1,0:T(8,128)S(1)}, u32[]{:S(2)}, u32[]{:S(2)}) collective-permute-start(f32[8,16,512]{2,1,0:T(8,128)S(1)} %pad_maximum_fusion.own_ref), channel_id=1, source_target_pairs={{0,63},{1,0},{2,1},{3,2},{4,3},{5,4},{6,5},{7,6},{8,7},{9,8},{10,9... | collective-permute-start | bytes 786440 | tf_op jit(solution)/shard_map/ppermute | solution.py:26
  46.4 0.6 longitude_kernel.1
  47.0 0.0 collective-permute-done.4.low_ref
  47.0 0.0 collective-permute-done.5.high_ref
  47.0 1.1 blend.1
  48.1 0.2 reshape.25
  48.3 0.7 copy.10
  49.0 5.5 %all-to-all-start.1 = ((f32[16,4,4,90]{3,2,1,0:T(4,128)}), f32[16,4,4,90]{3,2,1,0:T(4,128)S(1)}, u32[]{:S(2)}, u32[]{:S(2)}) async-start(f32[16,4,4,90]{3,2,1,0:T(4,128)} %bitcast.10), calls=%async_computation.1 | async-start | bytes 262144 | tf_op jit(solution)/shard_map/all_to_all | solution.py:214
  54.5 0.0 collective-permute-done.2.low_ref
  54.5 0.0 collective-permute-done.3.high_ref
  54.5 6.5 %diffuse.1 = f32[4,16,360]{2,1,0:T(8,128)S(1)} custom-call(f32[8,16,512]{2,1,0:T(8,128)S(1)} %collective-permute-done.2.low_ref, f32[8,16,512]{2,1,0:T(8,128)S(1)} %pad_maximum_fusion.own_ref, f32[8,16,512]{2,1,0:T(8,128)S(1)} %collective-permute-done.3.high_ref), custom_call_target="tpu_custom_call" | custom-call | flops 18874368 | bytes 2097152 | tf_op jit(solution)/shard_map/diffuse/pallas_call | solution.py:170
  61.0 1.0 all-to-all-done.1
  62.0 0.2 fusion.1
  62.3 0.0 copy-start.3
  62.3 1.3 multiply_reduce_fusion.1
  63.6 118.2 %all-reduce = (f32[]{:T(128)}, f32[]{:T(128)}) all-reduce(f32[]{:T(128)} %get-tuple-element.7, f32[]{:T(128)} %get-tuple-element.6), channel_id=1, replica_groups=mesh['mem_0'=2,'mem_1'=8,'band_0'=4,'band_1'=8,'band_2'=2] {'mem_0','mem..., use_global_device_ids=true, to_apply=%region_4.5 | all-reduce | flops 2 | bytes 16 | tf_op jit(solution)/shard_map/psum | solution.py:228
  183.7 0.0 copy-done.3
  183.7 0.7 multiply_subtract_fusion
  (9 shorter events, 0.2 us)
Async XLA Ops:
  2.7 9.3 %copy-start.1 = (f32[4,16,360]{2,1,0:T(8,128)S(1)}, f32[4,16,360]{2,1,0:T(8,128)}, u32[]{:S(2)}) copy-start(f32[4,16,360]{2,1,0:T(8,128)} %param.5) | copy-start | bytes 276484
  2.7 17.8 %all-to-all-start = ((f32[16,4,4,90]{3,2,1,0:T(4,128)}), f32[16,4,4,90]{3,2,1,0:T(4,128)S(1)}, u32[]{:S(2)}, u32[]{:S(2)}) async-start(f32[16,4,4,90]{3,2,1,0:T(4,128)} %broadcast_in_dim.17), calls=%async_computation | async-start | bytes 262144 | tf_op jit(solution)/shard_map/all_to_all | solution.py:31
  11.9 0.9 copy-start.2
  12.9 7.8 %copy-start = (f32[4,4,4,1440]{3,2,1,0:T(4,128)S(1)}, f32[4,4,4,1440]{3,2,1,0:T(4,128)}, u32[]{:S(2)}) copy-start(f32[4,4,4,1440]{3,2,1,0:T(4,128)} %ensemble_ref.1) | copy-start | bytes 1105924
  12.9 20.7 %collective-permute-start = (f32[8,16,16]{2,1,0:T(8,128)S(1)}, f32[8,16,16]{2,1,0:T(8,128)S(1)}, u32[]{:S(2)}, u32[]{:S(2)}) collective-permute-start(f32[8,16,16]{2,1,0:T(8,128)S(1)} %get-tuple-element.12), channel_id=1, source_target_pairs={{0,960},{64,0},{128,64},{192,128},{256,192},{320,256},{384,320},{4... | collective-permute-start | bytes 24584 | tf_op jit(solution)/shard_map/ppermute | solution.py:26
  18.5 15.2 %collective-permute-start.1 = (f32[8,16,16]{2,1,0:T(8,128)S(1)}, f32[8,16,16]{2,1,0:T(8,128)S(1)}, u32[]{:S(2)}, u32[]{:S(2)}) collective-permute-start(f32[8,16,16]{2,1,0:T(8,128)S(1)} %get-tuple-element.13), channel_id=1, source_target_pairs={{0,64},{64,128},{128,192},{192,256},{256,320},{320,384},{384,448},... | collective-permute-start | bytes 24584 | tf_op jit(solution)/shard_map/ppermute | solution.py:26
  20.8 26.3 %collective-permute-start.4 = (f32[4,4,1440]{2,1,0:T(4,128)S(1)}, f32[4,4,1440]{2,1,0:T(4,128)S(1)}, u32[]{:S(2)}, u32[]{:S(2)}) collective-permute-start(f32[4,4,1440]{2,1,0:T(4,128)S(1)} %multiply_reduce_fusion.own_ref), channel_id=1, source_target_pairs={{0,1},{1,2},{2,3},{3,4},{4,5},{5,6},{6,7},{7,8},{8,9},{9,10},{10,1... | collective-permute-start | bytes 276488 | tf_op jit(solution)/shard_map/ppermute | solution.py:26
  27.1 19.9 %collective-permute-start.5 = (f32[4,4,1440]{2,1,0:T(4,128)S(1)}, f32[4,4,1440]{2,1,0:T(4,128)S(1)}, u32[]{:S(2)}, u32[]{:S(2)}) collective-permute-start(f32[4,4,1440]{2,1,0:T(4,128)S(1)} %multiply_reduce_fusion.own_ref), channel_id=1, source_target_pairs={{0,63},{1,0},{2,1},{3,2},{4,3},{5,4},{6,5},{7,6},{8,7},{9,8},{10,9... | collective-permute-start | bytes 276488 | tf_op jit(solution)/shard_map/ppermute | solution.py:26
  33.8 20.7 %collective-permute-start.2 = (f32[8,16,512]{2,1,0:T(8,128)S(1)}, f32[8,16,512]{2,1,0:T(8,128)S(1)}, u32[]{:S(2)}, u32[]{:S(2)}) collective-permute-start(f32[8,16,512]{2,1,0:T(8,128)S(1)} %pad_maximum_fusion.own_ref), channel_id=1, source_target_pairs={{0,1},{1,2},{2,3},{3,4},{4,5},{5,6},{6,7},{7,8},{8,9},{9,10},{10,1... | collective-permute-start | bytes 786440 | tf_op jit(solution)/shard_map/ppermute | solution.py:26
  35.7 18.8 %collective-permute-start.3 = (f32[8,16,512]{2,1,0:T(8,128)S(1)}, f32[8,16,512]{2,1,0:T(8,128)S(1)}, u32[]{:S(2)}, u32[]{:S(2)}) collective-permute-start(f32[8,16,512]{2,1,0:T(8,128)S(1)} %pad_maximum_fusion.own_ref), channel_id=1, source_target_pairs={{0,63},{1,0},{2,1},{3,2},{4,3},{5,4},{6,5},{7,6},{8,7},{9,8},{10,9... | collective-permute-start | bytes 786440 | tf_op jit(solution)/shard_map/ppermute | solution.py:26
  49.0 13.0 %all-to-all-start.1 = ((f32[16,4,4,90]{3,2,1,0:T(4,128)}), f32[16,4,4,90]{3,2,1,0:T(4,128)S(1)}, u32[]{:S(2)}, u32[]{:S(2)}) async-start(f32[16,4,4,90]{3,2,1,0:T(4,128)} %bitcast.10), calls=%async_computation.1 | async-start | bytes 262144 | tf_op jit(solution)/shard_map/all_to_all | solution.py:214
  62.3 121.4 %copy-start.3 = (f32[4,16,360]{2,1,0:T(8,128)S(1)}, f32[4,16,360]{2,1,0:T(8,128)}, u32[]{:S(2)}) copy-start(f32[4,16,360]{2,1,0:T(8,128)} %param.6) | copy-start | bytes 276484

commit v2 on v1

--- a/solution.py
+++ b/solution.py
@@ -13,7 +13,6 @@
 LOCLON = 48
 BAND = ("band_0", "band_1", "band_2")
 MEM = ("mem_0", "mem_1")
-ALL = ("mem_0", "mem_1", "band_0", "band_1", "band_2")
 
 LATITUDE_RATE = 0.25
 HYBRID_WEIGHT = 0.5
@@ -29,6 +28,12 @@
 def everywhere(shard, axis):
     copies = jnp.broadcast_to(shard[None], (lax.axis_size(axis), *shard.shape))
     return lax.all_to_all(copies, axis, split_axis=0, concat_axis=0, tiled=True)
+
+
+def summed_over(sums, groups):
+    for group in groups:
+        sums = everywhere(sums, group).sum(axis=0)
+    return sums
 
 
 def params():
@@ -225,8 +230,8 @@
         (variables, coarse_rows, REFINE, columns),
     ).reshape(gradient.shape)
     direction = HYBRID_WEIGHT * smoothed + HYBRID_WEIGHT * injected
-    along_sum, square_sum = lax.psum(
-        (jnp.sum(gradient * direction), jnp.sum(direction * direction)), ALL
+    along_sum, square_sum = summed_over(
+        jnp.stack([jnp.sum(gradient * direction), jnp.sum(direction * direction)]), (MEM, BAND)
     )
     analysis = previous - along_sum / (along_sum + square_sum) * direction
     return (analysis, direction)

time: 185 us -> 107 us (0.58)
  blocking collectives: 118 us -> 38.1 us
    psum x1 -> x0, blocking collectives: 118 us -> none  [shards(): lax.psum((jnp.sum(gradient * direction), jnp.sum(direction * direction)),...]
    all_to_all x0 -> x2, blocking collectives: none -> 38.1 us  [everywhere(): return lax.all_to_all(copies, axis, split_axis=0, concat_axis=0, tiled=True)]
  transfers between devices with their start and end apart: 8 -> 8, of which waited for: 1 -> 1; matrix products, arithmetic and copies ran while one was open for 1% -> 1% of each run, Pallas kernels for 4% -> 8%
where the time goes in v2:
time: 107 us
  starting transfers between devices  47.7 us (45%)
  blocking collectives  38.1 us (36%)
  Pallas kernels  8.16 us (8%)
  local copies, waits for them, and re-layouts  4.35 us (4%)
  other arithmetic  3.89 us (4%)
  between operations  2.94 us (3%)
    all_to_all x2, blocking collectives, everywhere(): return lax.all_to_all(copies, axis, split_axis=0, concat_axis=0, tiled=True)  38.1 us
    ppermute x6, starting transfers between devices, shifted(): lax.ppermute(block, axis, [(i, (i + step) % count) for i in range(count)])  32.9 us
    all_to_all x1, starting transfers between devices, everywhere(): return lax.all_to_all(copies, axis, split_axis=0, concat_axis=0, tiled=True)  9.26 us
    pallas_call x1, Pallas kernels, diffuse(): pl.pallas_call(diffuse_body, out_shape=jax.ShapeDtypeStruct((variables, t...  6.5 us
    all_to_all x1, starting transfers between devices, shards(): lax.all_to_all(blocks, MEM, split_axis=0, concat_axis=0, tiled=True)  5.53 us
  transfers between devices with their start and end apart: 8, of which 1 were waited for; matrix products, arithmetic and copies ran while one was open for 1% of the time, Pallas kernels for 8%

profile of v2, /device:TPU:1, one launch (start us, length us, event | category | flops | bytes accessed | tf_op | source)
XLA Modules:
  0.0 106.7 jit_solution(6828224646124063661)
XLA Ops:
  0.7 0.9 reshape.36
  1.6 0.1 reduce_sum.63
  1.6 0.4 convolution_multiply_fusion
  2.0 0.7 broadcast_in_dim.14
  2.7 0.0 copy-start.1
  2.7 9.3 %all-to-all-start = ((f32[16,4,4,90]{3,2,1,0:T(4,128)}), f32[16,4,4,90]{3,2,1,0:T(4,128)S(1)}, u32[]{:S(2)}, u32[]{:S(2)}) async-start(f32[16,4,4,90]{3,2,1,0:T(4,128)} %broadcast_in_dim.14), calls=%async_computation | async-start | bytes 262144 | tf_op jit(solution)/shard_map/all_to_all | solution.py:30
  11.9 0.0 copy-done.1
  11.9 0.0 copy-start.2
  12.0 0.9 copy-done.2
  12.9 0.0 copy-start
  12.9 0.1 fusion.15
  12.9 5.5 %collective-permute-start = (f32[8,16,16]{2,1,0:T(8,128)S(1)}, f32[8,16,16]{2,1,0:T(8,128)S(1)}, u32[]{:S(2)}, u32[]{:S(2)}) collective-permute-start(f32[8,16,16]{2,1,0:T(8,128)S(1)} %get-tuple-element.10), channel_id=1, source_target_pairs={{0,960},{64,0},{128,64},{192,128},{256,192},{320,256},{384,320},{4... | collective-permute-start | bytes 24584 | tf_op jit(solution)/shard_map/ppermute | solution.py:25
  18.5 1.9 %collective-permute-start.1 = (f32[8,16,16]{2,1,0:T(8,128)S(1)}, f32[8,16,16]{2,1,0:T(8,128)S(1)}, u32[]{:S(2)}, u32[]{:S(2)}) collective-permute-start(f32[8,16,16]{2,1,0:T(8,128)S(1)} %get-tuple-element.11), channel_id=1, source_target_pairs={{0,64},{64,128},{128,192},{192,256},{256,320},{320,384},{384,448},... | collective-permute-start | bytes 24584 | tf_op jit(solution)/shard_map/ppermute | solution.py:25
  20.4 0.1 pad.4.clone
  20.5 0.0 all-to-all-done
  20.5 0.1 mul.44
  20.7 0.0 copy-done
  20.7 0.1 multiply_reduce_fusion.own_ref
  20.8 6.3 %collective-permute-start.4 = (f32[4,4,1440]{2,1,0:T(4,128)S(1)}, f32[4,4,1440]{2,1,0:T(4,128)S(1)}, u32[]{:S(2)}, u32[]{:S(2)}) collective-permute-start(f32[4,4,1440]{2,1,0:T(4,128)S(1)} %multiply_reduce_fusion.own_ref), channel_id=1, source_target_pairs={{0,1},{1,2},{2,3},{3,4},{4,5},{5,6},{6,7},{7,8},{8,9},{9,10},{10,1... | collective-permute-start | bytes 276488 | tf_op jit(solution)/shard_map/ppermute | solution.py:25
  27.1 6.5 %collective-permute-start.5 = (f32[4,4,1440]{2,1,0:T(4,128)S(1)}, f32[4,4,1440]{2,1,0:T(4,128)S(1)}, u32[]{:S(2)}, u32[]{:S(2)}) collective-permute-start(f32[4,4,1440]{2,1,0:T(4,128)S(1)} %multiply_reduce_fusion.own_ref), channel_id=1, source_target_pairs={{0,63},{1,0},{2,1},{3,2},{4,3},{5,4},{6,5},{7,6},{8,7},{9,8},{10,9... | collective-permute-start | bytes 276488 | tf_op jit(solution)/shard_map/ppermute | solution.py:25
  33.6 0.0 collective-permute-done
  33.7 0.0 collective-permute-done.1
  33.7 0.1 pad_maximum_fusion.own_ref
  33.8 1.9 %collective-permute-start.2 = (f32[8,16,512]{2,1,0:T(8,128)S(1)}, f32[8,16,512]{2,1,0:T(8,128)S(1)}, u32[]{:S(2)}, u32[]{:S(2)}) collective-permute-start(f32[8,16,512]{2,1,0:T(8,128)S(1)} %pad_maximum_fusion.own_ref), channel_id=1, source_target_pairs={{0,1},{1,2},{2,3},{3,4},{4,5},{5,6},{6,7},{7,8},{8,9},{9,10},{10,1... | collective-permute-start | bytes 786440 | tf_op jit(solution)/shard_map/ppermute | solution.py:25
  35.7 10.7 %collective-permute-start.3 = (f32[8,16,512]{2,1,0:T(8,128)S(1)}, f32[8,16,512]{2,1,0:T(8,128)S(1)}, u32[]{:S(2)}, u32[]{:S(2)}) collective-permute-start(f32[8,16,512]{2,1,0:T(8,128)S(1)} %pad_maximum_fusion.own_ref), channel_id=1, source_target_pairs={{0,63},{1,0},{2,1},{3,2},{4,3},{5,4},{6,5},{7,6},{8,7},{9,8},{10,9... | collective-permute-start | bytes 786440 | tf_op jit(solution)/shard_map/ppermute | solution.py:25
  46.4 0.6 longitude_kernel.1
  47.0 0.0 collective-permute-done.4.low_ref
  47.0 0.0 collective-permute-done.5.high_ref
  47.0 1.1 blend.1
  48.1 0.2 reshape.37
  48.3 0.7 copy.20
  49.0 5.5 %all-to-all-start.1 = ((f32[16,4,4,90]{3,2,1,0:T(4,128)}), f32[16,4,4,90]{3,2,1,0:T(4,128)S(1)}, u32[]{:S(2)}, u32[]{:S(2)}) async-start(f32[16,4,4,90]{3,2,1,0:T(4,128)} %bitcast.14), calls=%async_computation.1 | async-start | bytes 262144 | tf_op jit(solution)/shard_map/all_to_all | solution.py:219
  54.5 0.0 collective-permute-done.2.low_ref
  54.5 0.0 collective-permute-done.3.high_ref
  54.5 6.5 %diffuse.1 = f32[4,16,360]{2,1,0:T(8,128)S(1)} custom-call(f32[8,16,512]{2,1,0:T(8,128)S(1)} %collective-permute-done.2.low_ref, f32[8,16,512]{2,1,0:T(8,128)S(1)} %pad_maximum_fusion.own_ref, f32[8,16,512]{2,1,0:T(8,128)S(1)} %collective-permute-done.3.high_ref), custom_call_target="tpu_custom_call" | custom-call | flops 18874368 | bytes 2097152 | tf_op jit(solution)/shard_map/diffuse/pallas_call | solution.py:175
  61.0 1.0 all-to-all-done.1
  62.0 0.2 fusion.1
  62.3 1.3 %multiply_reduce_fusion.2 = (f32[]{:T(128)}, f32[]{:T(128)}, f32[4,16,360]{2,1,0:T(8,128)}, f32[4,16,360]{2,1,0:T(8,128)S(1)}) fusion(f32[4,16,360]{2,1,0:T(8,128)S(1)} %copy-done.1, f32[4,16,360]{2,1,0:T(8,128)S(1)} %diffuse.1, f32[4,16,360]{2,1,0:T(8,128)S(1)} %reshape.38), kind=kLoop, calls=%fused_computation.10 | loop fusion | flops 138238 | bytes 460808 | tf_op jit(solution)/shard_map/reduce_sum | solution.py:234
  63.6 0.0 copy-start.3
  63.6 1.4 %pad_maximum_fusion.1 = f32[2]{0:T(128)S(1)} fusion(f32[1]{0:T(128)} %bitcast.5, f32[1]{0:T(128)} %bitcast.4), kind=kLoop, calls=%fused_computation.29 | loop fusion | flops 2 | bytes 16 | tf_op jit(solution)/shard_map/stack | solution.py:234
  65.1 13.7 %all_to_all.22 = f32[16,1,2]{2,1,0:T(1,128)S(1)} all-to-all(f32[16,1,2]{2,1,0:T(1,128)S(1)} %broadcast_in_dim.31), channel_id=1, replica_groups=mesh['mem_0'=2,'mem_1'=8,'band_0'=4,'band_1'=8,'band_2'=2] {'mem_0','mem..., dimensions={0} | all-to-all | bytes 256 | tf_op jit(solution)/shard_map/all_to_all | solution.py:30
  78.9 24.4 %all_to_all.23 = f32[64,1,2]{2,1,0:T(1,128)S(1)} all-to-all(f32[64,1,2]{2,1,0:T(1,128)S(1)} %broadcast_in_dim.32), channel_id=1, replica_groups=mesh['mem_0'=2,'mem_1'=8,'band_0'=4,'band_1'=8,'band_2'=2] {'band_0','ba..., dimensions={0} | all-to-all | bytes 1024 | tf_op jit(solution)/shard_map/all_to_all | solution.py:30
  103.3 0.1 reduce_sum.69
  103.4 0.6 fusion.16
  106.0 0.0 copy-done.3
  106.0 0.7 multiply_subtract_fusion
  (12 shorter events, 0.2 us)
Async XLA Ops:
  2.7 9.3 %copy-start.1 = (f32[4,16,360]{2,1,0:T(8,128)S(1)}, f32[4,16,360]{2,1,0:T(8,128)}, u32[]{:S(2)}) copy-start(f32[4,16,360]{2,1,0:T(8,128)} %param.5) | copy-start | bytes 276484
  2.7 17.8 %all-to-all-start = ((f32[16,4,4,90]{3,2,1,0:T(4,128)}), f32[16,4,4,90]{3,2,1,0:T(4,128)S(1)}, u32[]{:S(2)}, u32[]{:S(2)}) async-start(f32[16,4,4,90]{3,2,1,0:T(4,128)} %broadcast_in_dim.14), calls=%async_computation | async-start | bytes 262144 | tf_op jit(solution)/shard_map/all_to_all | solution.py:30
  11.9 0.9 copy-start.2
  12.9 7.8 %copy-start = (f32[4,4,4,1440]{3,2,1,0:T(4,128)S(1)}, f32[4,4,4,1440]{3,2,1,0:T(4,128)}, u32[]{:S(2)}) copy-start(f32[4,4,4,1440]{3,2,1,0:T(4,128)} %ensemble_ref.1) | copy-start | bytes 1105924
  12.9 20.7 %collective-permute-start = (f32[8,16,16]{2,1,0:T(8,128)S(1)}, f32[8,16,16]{2,1,0:T(8,128)S(1)}, u32[]{:S(2)}, u32[]{:S(2)}) collective-permute-start(f32[8,16,16]{2,1,0:T(8,128)S(1)} %get-tuple-element.10), channel_id=1, source_target_pairs={{0,960},{64,0},{128,64},{192,128},{256,192},{320,256},{384,320},{4... | collective-permute-start | bytes 24584 | tf_op jit(solution)/shard_map/ppermute | solution.py:25
  18.5 15.2 %collective-permute-start.1 = (f32[8,16,16]{2,1,0:T(8,128)S(1)}, f32[8,16,16]{2,1,0:T(8,128)S(1)}, u32[]{:S(2)}, u32[]{:S(2)}) collective-permute-start(f32[8,16,16]{2,1,0:T(8,128)S(1)} %get-tuple-element.11), channel_id=1, source_target_pairs={{0,64},{64,128},{128,192},{192,256},{256,320},{320,384},{384,448},... | collective-permute-start | bytes 24584 | tf_op jit(solution)/shard_map/ppermute | solution.py:25
  20.8 26.3 %collective-permute-start.4 = (f32[4,4,1440]{2,1,0:T(4,128)S(1)}, f32[4,4,1440]{2,1,0:T(4,128)S(1)}, u32[]{:S(2)}, u32[]{:S(2)}) collective-permute-start(f32[4,4,1440]{2,1,0:T(4,128)S(1)} %multiply_reduce_fusion.own_ref), channel_id=1, source_target_pairs={{0,1},{1,2},{2,3},{3,4},{4,5},{5,6},{6,7},{7,8},{8,9},{9,10},{10,1... | collective-permute-start | bytes 276488 | tf_op jit(solution)/shard_map/ppermute | solution.py:25
  27.1 19.9 %collective-permute-start.5 = (f32[4,4,1440]{2,1,0:T(4,128)S(1)}, f32[4,4,1440]{2,1,0:T(4,128)S(1)}, u32[]{:S(2)}, u32[]{:S(2)}) collective-permute-start(f32[4,4,1440]{2,1,0:T(4,128)S(1)} %multiply_reduce_fusion.own_ref), channel_id=1, source_target_pairs={{0,63},{1,0},{2,1},{3,2},{4,3},{5,4},{6,5},{7,6},{8,7},{9,8},{10,9... | collective-permute-start | bytes 276488 | tf_op jit(solution)/shard_map/ppermute | solution.py:25
  33.8 20.7 %collective-permute-start.2 = (f32[8,16,512]{2,1,0:T(8,128)S(1)}, f32[8,16,512]{2,1,0:T(8,128)S(1)}, u32[]{:S(2)}, u32[]{:S(2)}) collective-permute-start(f32[8,16,512]{2,1,0:T(8,128)S(1)} %pad_maximum_fusion.own_ref), channel_id=1, source_target_pairs={{0,1},{1,2},{2,3},{3,4},{4,5},{5,6},{6,7},{7,8},{8,9},{9,10},{10,1... | collective-permute-start | bytes 786440 | tf_op jit(solution)/shard_map/ppermute | solution.py:25
  35.7 18.8 %collective-permute-start.3 = (f32[8,16,512]{2,1,0:T(8,128)S(1)}, f32[8,16,512]{2,1,0:T(8,128)S(1)}, u32[]{:S(2)}, u32[]{:S(2)}) collective-permute-start(f32[8,16,512]{2,1,0:T(8,128)S(1)} %pad_maximum_fusion.own_ref), channel_id=1, source_target_pairs={{0,63},{1,0},{2,1},{3,2},{4,3},{5,4},{6,5},{7,6},{8,7},{9,8},{10,9... | collective-permute-start | bytes 786440 | tf_op jit(solution)/shard_map/ppermute | solution.py:25
  49.0 13.0 %all-to-all-start.1 = ((f32[16,4,4,90]{3,2,1,0:T(4,128)}), f32[16,4,4,90]{3,2,1,0:T(4,128)S(1)}, u32[]{:S(2)}, u32[]{:S(2)}) async-start(f32[16,4,4,90]{3,2,1,0:T(4,128)} %bitcast.14), calls=%async_computation.1 | async-start | bytes 262144 | tf_op jit(solution)/shard_map/all_to_all | solution.py:219
  63.6 42.4 %copy-start.3 = (f32[4,16,360]{2,1,0:T(8,128)S(1)}, f32[4,16,360]{2,1,0:T(8,128)}, u32[]{:S(2)}) copy-start(f32[4,16,360]{2,1,0:T(8,128)} %param.6) | copy-start | bytes 276484

commit v3 on v1

--- a/solution.py
+++ b/solution.py
@@ -1,3 +1,5 @@
+import functools
+
 import jax
 import jax.numpy as jnp
 from jax import lax
@@ -13,7 +15,8 @@
 LOCLON = 48
 BAND = ("band_0", "band_1", "band_2")
 MEM = ("mem_0", "mem_1")
-ALL = ("mem_0", "mem_1", "band_0", "band_1", "band_2")
+NEAR = ("mem_0", "mem_1", "band_2")
+FAR = ("band_0", "band_1")
 
 LATITUDE_RATE = 0.25
 HYBRID_WEIGHT = 0.5
@@ -148,17 +151,20 @@
         east_ref[v] = jnp.sqrt(rate * pltpu.roll(rate, width - 1, 1))
         north_ref[v] = jnp.where(inside, jnp.sqrt(rate * pltpu.roll(rate, height - 1, 0)), 0.0)
 
-    def substep(_, carry):
-        for v in range(variables):
-            f = field_ref[v]
-            east = east_ref[v] * (pltpu.roll(f, width - 1, 1) - f)
-            north = north_ref[v] * (pltpu.roll(f, height - 1, 0) - f)
-            change = east - pltpu.roll(east, 1, 1)
-            change = change + north - pltpu.roll(north, 1, 0)
-            field_ref[v] = f + change
-        return carry
-
-    lax.fori_loop(0, SUBSTEPS, substep, 0)
+    half = SUBSTEPS // 2
+    for low, high in ((0, height), (half, height - half)):
+
+        def substep(_, carry, low=low, high=high):
+            for v in range(variables):
+                f = field_ref[v, low:high]
+                east = east_ref[v, low:high] * (pltpu.roll(f, width - 1, 1) - f)
+                north = north_ref[v, low:high] * (pltpu.roll(f, high - low - 1, 0) - f)
+                change = east - pltpu.roll(east, 1, 1)
+                change = change + north - pltpu.roll(north, 1, 0)
+                field_ref[v, low:high] = f + change
+            return carry
+
+        lax.fori_loop(0, half, substep, 0)
     for v in range(variables):
         out_ref[v] = field_ref[v, tile_rows : 2 * tile_rows, : out_ref.shape[2]]
 
@@ -179,11 +185,77 @@
     )(low, own, high)
 
 
-def chosen(rows, columns, ratio, by_row):
+def chosen(rows, columns):
     own = lax.broadcasted_iota(jnp.int32, (rows, columns), 0)
     other = lax.broadcasted_iota(jnp.int32, (rows, columns), 1)
-    same = (other // ratio == own) if by_row else (own // ratio == other)
-    return same.astype(jnp.float32)
+    return (own // REFINE == other).astype(jnp.float32)
+
+
+def combine_body(inverse_count, arrived_ref, smoothed_ref, gradient_ref, direction_ref, sums_ref):
+    owners, variables, coarse_rows, coarse_cols = arrived_ref.shape
+    columns = smoothed_ref.shape[2]
+    part = arrived_ref[0]
+    for k in range(1, owners):
+        part = part + arrived_ref[k]
+    part = jnp.concatenate([part[v] for v in range(variables)], axis=0) * inverse_count
+    own = lax.broadcasted_iota(jnp.int32, (coarse_cols, columns), 0)
+    other = lax.broadcasted_iota(jnp.int32, (coarse_cols, columns), 1)
+    copies = jnp.where(lax.shift_right_logical(other, 2) == own, 1.0, 0.0)
+    spread = jnp.dot(
+        part, copies, precision=lax.Precision.HIGHEST, preferred_element_type=jnp.float32
+    )
+    along = jnp.zeros((coarse_rows * REFINE, columns), jnp.float32)
+    square = along
+    for v in range(variables):
+        injected = jnp.concatenate(
+            [
+                jnp.broadcast_to(spread[i : i + 1], (REFINE, columns))
+                for i in range(v * coarse_rows, (v + 1) * coarse_rows)
+            ],
+            axis=0,
+        )
+        direction = HYBRID_WEIGHT * smoothed_ref[v] + HYBRID_WEIGHT * injected
+        direction_ref[v] = direction
+        along = along + gradient_ref[v] * direction
+        square = square + direction * direction
+    along = jnp.sum(jnp.sum(along, axis=0, keepdims=True), axis=1, keepdims=True)
+    square = jnp.sum(jnp.sum(square, axis=0, keepdims=True), axis=1, keepdims=True)
+    lane = lax.broadcasted_iota(jnp.int32, sums_ref.shape, 1)
+    sums_ref[...] = jnp.where(lane == 0, along, jnp.where(lane == 1, square, 0.0))
+
+
+def combine(arrived, smoothed, gradient, inverse_count, peers):
+    return pl.pallas_call(
+        functools.partial(combine_body, inverse_count),
+        out_shape=(
+            jax.ShapeDtypeStruct(gradient.shape, jnp.float32),
+            jax.ShapeDtypeStruct((peers, 128), jnp.float32),
+        ),
+        compiler_params=params(),
+        cost_estimate=pl.CostEstimate(flops=8 << 20, transcendentals=0, bytes_accessed=1 << 20),
+        name="combine",
+    )(arrived, smoothed, gradient)
+
+
+def step_body(sums_ref, direction_ref, previous_ref, analysis_ref, out_ref):
+    sums = jnp.sum(sums_ref[...], axis=0, keepdims=True)
+    along, square = sums[:, 0:1], sums[:, 1:2]
+    length = along / (along + square)
+    for v in range(direction_ref.shape[0]):
+        direction = direction_ref[v]
+        out_ref[v] = direction
+        analysis_ref[v] = previous_ref[v] - length * direction
+
+
+def step(sums, direction, previous):
+    tile = jax.ShapeDtypeStruct(direction.shape, jnp.float32)
+    return pl.pallas_call(
+        step_body,
+        out_shape=(tile, tile),
+        compiler_params=params(),
+        cost_estimate=pl.CostEstimate(flops=1 << 20, transcendentals=0, bytes_accessed=1 << 20),
+        name="step",
+    )(sums, direction, previous)
 
 
 def shards(ensemble, gradient, previous, diffusivity):
@@ -193,7 +265,7 @@
     owners = lax.axis_size(MEM)
     row_sums = gradient.reshape(variables * coarse_rows, REFINE, columns).sum(axis=1)
     restricted = jnp.dot(
-        row_sums, chosen(columns, coarse_cols, REFINE, False), precision=lax.Precision.HIGHEST
+        row_sums, chosen(columns, coarse_cols), precision=lax.Precision.HIGHEST
     ) * (1.0 / (REFINE * REFINE))
     gathered = everywhere(restricted.reshape(variables, coarse_rows, coarse_cols), MEM)
     gathered = jnp.moveaxis(gathered, 0, 2).reshape(variables, coarse_rows, NLON)
@@ -213,23 +285,13 @@
     blocks = jnp.moveaxis(member_terms.reshape(variables, coarse_rows, owners, coarse_cols), 2, 0)
     arrived = lax.all_to_all(blocks, MEM, split_axis=0, concat_axis=0, tiled=True)
     smoothed = diffuse(rows_low, extended, rows_high, columns)
-    inverse_count = 1.0 / (members * owners - 1)
-    ensemble_part = arrived.sum(axis=0) * inverse_count
-    spread = jnp.dot(
-        ensemble_part.reshape(variables * coarse_rows, coarse_cols),
-        chosen(coarse_cols, columns, REFINE, True),
-        precision=lax.Precision.HIGHEST,
-    )
-    injected = jnp.broadcast_to(
-        spread.reshape(variables, coarse_rows, 1, columns),
-        (variables, coarse_rows, REFINE, columns),
-    ).reshape(gradient.shape)
-    direction = HYBRID_WEIGHT * smoothed + HYBRID_WEIGHT * injected
-    along_sum, square_sum = lax.psum(
-        (jnp.sum(gradient * direction), jnp.sum(direction * direction)), ALL
-    )
-    analysis = previous - along_sum / (along_sum + square_sum) * direction
-    return (analysis, direction)
+    peers = lax.axis_size(NEAR)
+    direction, sums = combine(
+        arrived, smoothed, gradient, 1.0 / (members * owners - 1), peers
+    )
+    sums = lax.all_to_all(sums, NEAR, split_axis=0, concat_axis=0, tiled=True)
+    sums = everywhere(sums.sum(axis=0, keepdims=True), FAR)
+    return step(sums.reshape(-1, 128), direction, previous)
 
 
 def solution(mesh):

time: 185 us -> 101 us (0.55)
  blocking collectives: 118 us -> 35.6 us
  between operations: 2.83 us -> 0.87 us
  other arithmetic: 2.27 us -> 0.33 us
    psum x1 -> x0, blocking collectives: 118 us -> none  [shards(): lax.psum((jnp.sum(gradient * direction), jnp.sum(direction * direction)),...]
    all_to_all x0 -> x2, blocking collectives: none -> 35.6 us  [the longest x1 20.3 us: shards(): sums = lax.all_to_all(sums, NEAR, split_axis=0, concat_axis=0, tiled=True)]
  transfers between devices with their start and end apart: 8 -> 8, of which waited for: 1 -> 1; matrix products, arithmetic and copies ran while one was open for 1% -> 1% of each run, Pallas kernels for 4% -> 7%
where the time goes in v3:
time: 101 us; the launch traced here: 100 us
  starting transfers between devices  48.9 us (48%)
  blocking collectives  35.6 us (35%)
  Pallas kernels  8.28 us (8%)
  local copies, waits for them, and re-layouts  3.69 us (4%)
  waiting for transfers between devices  1.95 us (2%)
    ppermute x6, starting transfers between devices, shifted(): lax.ppermute(block, axis, [(i, (i + step) % count) for i in range(count)])  33 us
    all_to_all x1, blocking collectives, shards(): sums = lax.all_to_all(sums, NEAR, split_axis=0, concat_axis=0, tiled=True)  20.3 us
    all_to_all x1, blocking collectives, everywhere(): return lax.all_to_all(copies, axis, split_axis=0, concat_axis=0, tiled=True)  15.4 us
    all_to_all x1, starting transfers between devices, everywhere(): return lax.all_to_all(copies, axis, split_axis=0, concat_axis=0, tiled=True)  9.26 us
    all_to_all x1, starting transfers between devices, shards(): lax.all_to_all(blocks, MEM, split_axis=0, concat_axis=0, tiled=True)  6.66 us
    pallas_call x1, Pallas kernels, diffuse(): pl.pallas_call(diffuse_body, out_shape=jax.ShapeDtypeStruct((variables, t...  5.55 us
  transfers between devices with their start and end apart: 8, of which 1 were waited for; matrix products, arithmetic and copies ran while one was open for 1% of the time, Pallas kernels for 7%

profile of v3, /device:TPU:1, one launch (start us, length us, event | category | flops | bytes accessed | tf_op | source)
XLA Modules:
  0.0 100.0 jit_solution(3805702184435099293)
XLA Ops:
  0.7 0.9 reshape.20
  1.6 0.1 reduce_sum.27
  1.6 0.4 convolution_multiply_fusion
  2.0 0.7 broadcast_in_dim.16
  2.7 0.0 copy-start.1
  2.7 9.3 %all-to-all-start = ((f32[16,4,4,90]{3,2,1,0:T(4,128)}), f32[16,4,4,90]{3,2,1,0:T(4,128)S(1)}, u32[]{:S(2)}, u32[]{:S(2)}) async-start(f32[16,4,4,90]{3,2,1,0:T(4,128)} %broadcast_in_dim.16), calls=%async_computation | async-start | bytes 262144 | tf_op jit(solution)/shard_map/all_to_all | solution.py:34
  11.9 0.0 copy-done.1
  12.0 0.0 copy-start.3
  12.0 0.9 copy-done.3
  12.9 0.0 copy-start
  12.9 0.1 fusion.6
  13.0 3.4 %collective-permute-start.3 = (f32[8,16,16]{2,1,0:T(8,128)S(1)}, f32[8,16,16]{2,1,0:T(8,128)S(1)}, u32[]{:S(2)}, u32[]{:S(2)}) collective-permute-start(f32[8,16,16]{2,1,0:T(8,128)S(1)} %get-tuple-element.11), channel_id=1, source_target_pairs={{0,64},{64,128},{128,192},{192,256},{256,320},{320,384},{384,448},... | collective-permute-start | bytes 24584 | tf_op jit(solution)/shard_map/ppermute | solution.py:29
  16.4 4.1 %collective-permute-start.2 = (f32[8,16,16]{2,1,0:T(8,128)S(1)}, f32[8,16,16]{2,1,0:T(8,128)S(1)}, u32[]{:S(2)}, u32[]{:S(2)}) collective-permute-start(f32[8,16,16]{2,1,0:T(8,128)S(1)} %get-tuple-element.10), channel_id=1, source_target_pairs={{0,960},{64,0},{128,64},{192,128},{256,192},{320,256},{384,320},{4... | collective-permute-start | bytes 24584 | tf_op jit(solution)/shard_map/ppermute | solution.py:29
  20.5 0.1 pad.2.clone
  20.6 0.0 all-to-all-done
  20.6 0.1 mul.18
  20.8 0.0 copy-done
  20.8 0.1 multiply_reduce_fusion.own_ref
  20.9 6.3 %collective-permute-start = (f32[4,4,1440]{2,1,0:T(4,128)S(1)}, f32[4,4,1440]{2,1,0:T(4,128)S(1)}, u32[]{:S(2)}, u32[]{:S(2)}) collective-permute-start(f32[4,4,1440]{2,1,0:T(4,128)S(1)} %multiply_reduce_fusion.own_ref), channel_id=1, source_target_pairs={{0,1},{1,2},{2,3},{3,4},{4,5},{5,6},{6,7},{7,8},{8,9},{9,10},{10,1... | collective-permute-start | bytes 276488 | tf_op jit(solution)/shard_map/ppermute | solution.py:29
  27.2 6.6 %collective-permute-start.1 = (f32[4,4,1440]{2,1,0:T(4,128)S(1)}, f32[4,4,1440]{2,1,0:T(4,128)S(1)}, u32[]{:S(2)}, u32[]{:S(2)}) collective-permute-start(f32[4,4,1440]{2,1,0:T(4,128)S(1)} %multiply_reduce_fusion.own_ref), channel_id=1, source_target_pairs={{0,63},{1,0},{2,1},{3,2},{4,3},{5,4},{6,5},{7,6},{8,7},{9,8},{10,9... | collective-permute-start | bytes 276488 | tf_op jit(solution)/shard_map/ppermute | solution.py:29
  33.8 0.0 collective-permute-done.3
  33.8 0.0 collective-permute-done.2
  33.8 0.1 pad_maximum_fusion.own_ref
  33.9 1.9 %collective-permute-start.4 = (f32[8,16,512]{2,1,0:T(8,128)S(1)}, f32[8,16,512]{2,1,0:T(8,128)S(1)}, u32[]{:S(2)}, u32[]{:S(2)}) collective-permute-start(f32[8,16,512]{2,1,0:T(8,128)S(1)} %pad_maximum_fusion.own_ref), channel_id=1, source_target_pairs={{0,1},{1,2},{2,3},{3,4},{4,5},{5,6},{6,7},{7,8},{8,9},{9,10},{10,1... | collective-permute-start | bytes 786440 | tf_op jit(solution)/shard_map/ppermute | solution.py:29
  35.8 10.7 %collective-permute-start.5 = (f32[8,16,512]{2,1,0:T(8,128)S(1)}, f32[8,16,512]{2,1,0:T(8,128)S(1)}, u32[]{:S(2)}, u32[]{:S(2)}) collective-permute-start(f32[8,16,512]{2,1,0:T(8,128)S(1)} %pad_maximum_fusion.own_ref), channel_id=1, source_target_pairs={{0,63},{1,0},{2,1},{3,2},{4,3},{5,4},{6,5},{7,6},{8,7},{9,8},{10,9... | collective-permute-start | bytes 786440 | tf_op jit(solution)/shard_map/ppermute | solution.py:29
  46.5 0.6 longitude_kernel.1
  47.1 0.0 collective-permute-done.low_ref
  47.1 0.0 collective-permute-done.1.high_ref
  47.1 1.1 %blend.1 = f32[4,4,1440]{2,1,0:T(4,128)S(1)} custom-call(f32[4,4,4,1440]{3,2,1,0:T(4,128)S(1)} %copy-done, f32[4,4,1440]{2,1,0:T(4,128)S(1)} %collective-permute-done.low_ref, f32[4,4,1440]{2,1,0:T(4,128)S(1)} %multiply_reduce_fusion.own_ref, f32[4,4,1440]{2,1,0:T(4,128)S(1)} %collective-permute-done.1.high_ref, ...), custom_call_target="tpu_custom_call" | custom-call | flops 199065600 | bytes 4194304 | tf_op jit(solution)/shard_map/blend/pallas_call | solution.py:125
  48.2 0.2 reshape.21
  48.4 0.7 copy.13
  49.1 6.7 %all-to-all-start.1 = ((f32[16,4,4,90]{3,2,1,0:T(4,128)}), f32[16,4,4,90]{3,2,1,0:T(4,128)S(1)}, u32[]{:S(2)}, u32[]{:S(2)}) async-start(f32[16,4,4,90]{3,2,1,0:T(4,128)} %bitcast.11), calls=%async_computation.1 | async-start | bytes 262144 | tf_op jit(solution)/shard_map/all_to_all | solution.py:286
  55.7 0.0 collective-permute-done.4.low_ref
  55.7 0.0 collective-permute-done.5.high_ref
  55.7 5.5 %diffuse.1.smoothed_ref = f32[4,16,360]{2,1,0:T(8,128)S(1)} custom-call(f32[8,16,512]{2,1,0:T(8,128)S(1)} %collective-permute-done.4.low_ref, f32[8,16,512]{2,1,0:T(8,128)S(1)} %pad_maximum_fusion.own_ref, f32[8,16,512]{2,1,0:T(8,128)S(1)} %collective-permute-done.5.high_ref), custom_call_target="tpu_custom_call" | custom-call | flops 18874368 | bytes 2097152 | tf_op jit(solution)/shard_map/diffuse/pallas_call | solution.py:176
  61.3 1.9 %all-to-all-done.1.arrived_ref = f32[16,4,4,90]{3,2,1,0:T(4,128)S(1)} async-done(((f32[16,4,4,90]{3,2,1,0:T(4,128)}), f32[16,4,4,90]{3,2,1,0:T(4,128)S(1)}, u32[]{:S(2)}, u32[]{:S(2)}) %all-to-all-start.1) | async-done | bytes 92192 | tf_op jit(solution)/shard_map/all_to_all | solution.py:286
  63.2 0.3 combine.1
  63.5 0.0 copy-start.2
  63.5 20.3 %all_to_all.24 = f32[32,1,128]{2,1,0:T(1,128)S(1)} all-to-all(f32[32,1,128]{2,1,0:T(1,128)S(1)} %bitcast.13), channel_id=1, replica_groups=mesh['mem_0'=2,'mem_1'=8,'band_0'=4,'band_1'=8,'band_2'=2] {'mem_0','mem..., dimensions={0} | all-to-all | bytes 32768 | tf_op jit(solution)/shard_map/all_to_all | solution.py:292
  83.8 0.1 reduce_sum.29
  83.8 15.4 %all_to_all.25 = f32[32,1,128]{2,1,0:T(1,128)S(1)} all-to-all(f32[32,1,128]{2,1,0:T(1,128)S(1)} %broadcast_in_dim.18), channel_id=1, replica_groups=mesh['mem_0'=2,'mem_1'=8,'band_0'=4,'band_1'=8,'band_2'=2] {'band_0','ba..., dimensions={0} | all-to-all | bytes 32768 | tf_op jit(solution)/shard_map/all_to_all | solution.py:34
  99.2 0.0 copy-done.2
  99.2 0.8 step.1
  (7 shorter events, 0.1 us)
Async XLA Ops:
  2.7 9.3 %copy-start.1 = (f32[4,16,360]{2,1,0:T(8,128)S(1)}, f32[4,16,360]{2,1,0:T(8,128)}, u32[]{:S(2)}) copy-start(f32[4,16,360]{2,1,0:T(8,128)} %gradient_ref.1) | copy-start | bytes 276484
  2.7 17.9 %all-to-all-start = ((f32[16,4,4,90]{3,2,1,0:T(4,128)}), f32[16,4,4,90]{3,2,1,0:T(4,128)S(1)}, u32[]{:S(2)}, u32[]{:S(2)}) async-start(f32[16,4,4,90]{3,2,1,0:T(4,128)} %broadcast_in_dim.16), calls=%async_computation | async-start | bytes 262144 | tf_op jit(solution)/shard_map/all_to_all | solution.py:34
  12.0 0.9 copy-start.3
  12.9 7.9 %copy-start = (f32[4,4,4,1440]{3,2,1,0:T(4,128)S(1)}, f32[4,4,4,1440]{3,2,1,0:T(4,128)}, u32[]{:S(2)}) copy-start(f32[4,4,4,1440]{3,2,1,0:T(4,128)} %ensemble_ref.1) | copy-start | bytes 1105924
  13.0 20.8 %collective-permute-start.3 = (f32[8,16,16]{2,1,0:T(8,128)S(1)}, f32[8,16,16]{2,1,0:T(8,128)S(1)}, u32[]{:S(2)}, u32[]{:S(2)}) collective-permute-start(f32[8,16,16]{2,1,0:T(8,128)S(1)} %get-tuple-element.11), channel_id=1, source_target_pairs={{0,64},{64,128},{128,192},{192,256},{256,320},{320,384},{384,448},... | collective-permute-start | bytes 24584 | tf_op jit(solution)/shard_map/ppermute | solution.py:29
  16.4 17.4 %collective-permute-start.2 = (f32[8,16,16]{2,1,0:T(8,128)S(1)}, f32[8,16,16]{2,1,0:T(8,128)S(1)}, u32[]{:S(2)}, u32[]{:S(2)}) collective-permute-start(f32[8,16,16]{2,1,0:T(8,128)S(1)} %get-tuple-element.10), channel_id=1, source_target_pairs={{0,960},{64,0},{128,64},{192,128},{256,192},{320,256},{384,320},{4... | collective-permute-start | bytes 24584 | tf_op jit(solution)/shard_map/ppermute | solution.py:29
  20.9 26.3 %collective-permute-start = (f32[4,4,1440]{2,1,0:T(4,128)S(1)}, f32[4,4,1440]{2,1,0:T(4,128)S(1)}, u32[]{:S(2)}, u32[]{:S(2)}) collective-permute-start(f32[4,4,1440]{2,1,0:T(4,128)S(1)} %multiply_reduce_fusion.own_ref), channel_id=1, source_target_pairs={{0,1},{1,2},{2,3},{3,4},{4,5},{5,6},{6,7},{7,8},{8,9},{9,10},{10,1... | collective-permute-start | bytes 276488 | tf_op jit(solution)/shard_map/ppermute | solution.py:29
  27.2 19.9 %collective-permute-start.1 = (f32[4,4,1440]{2,1,0:T(4,128)S(1)}, f32[4,4,1440]{2,1,0:T(4,128)S(1)}, u32[]{:S(2)}, u32[]{:S(2)}) collective-permute-start(f32[4,4,1440]{2,1,0:T(4,128)S(1)} %multiply_reduce_fusion.own_ref), channel_id=1, source_target_pairs={{0,63},{1,0},{2,1},{3,2},{4,3},{5,4},{6,5},{7,6},{8,7},{9,8},{10,9... | collective-permute-start | bytes 276488 | tf_op jit(solution)/shard_map/ppermute | solution.py:29
  33.9 21.8 %collective-permute-start.4 = (f32[8,16,512]{2,1,0:T(8,128)S(1)}, f32[8,16,512]{2,1,0:T(8,128)S(1)}, u32[]{:S(2)}, u32[]{:S(2)}) collective-permute-start(f32[8,16,512]{2,1,0:T(8,128)S(1)} %pad_maximum_fusion.own_ref), channel_id=1, source_target_pairs={{0,1},{1,2},{2,3},{3,4},{4,5},{5,6},{6,7},{7,8},{8,9},{9,10},{10,1... | collective-permute-start | bytes 786440 | tf_op jit(solution)/shard_map/ppermute | solution.py:29
  35.8 19.9 %collective-permute-start.5 = (f32[8,16,512]{2,1,0:T(8,128)S(1)}, f32[8,16,512]{2,1,0:T(8,128)S(1)}, u32[]{:S(2)}, u32[]{:S(2)}) collective-permute-start(f32[8,16,512]{2,1,0:T(8,128)S(1)} %pad_maximum_fusion.own_ref), channel_id=1, source_target_pairs={{0,63},{1,0},{2,1},{3,2},{4,3},{5,4},{6,5},{7,6},{8,7},{9,8},{10,9... | collective-permute-start | bytes 786440 | tf_op jit(solution)/shard_map/ppermute | solution.py:29
  49.1 14.2 %all-to-all-start.1 = ((f32[16,4,4,90]{3,2,1,0:T(4,128)}), f32[16,4,4,90]{3,2,1,0:T(4,128)S(1)}, u32[]{:S(2)}, u32[]{:S(2)}) async-start(f32[16,4,4,90]{3,2,1,0:T(4,128)} %bitcast.11), calls=%async_computation.1 | async-start | bytes 262144 | tf_op jit(solution)/shard_map/all_to_all | solution.py:286
  63.5 35.7 %copy-start.2 = (f32[4,16,360]{2,1,0:T(8,128)S(1)}, f32[4,16,360]{2,1,0:T(8,128)}, u32[]{:S(2)}) copy-start(f32[4,16,360]{2,1,0:T(8,128)} %previous_ref.1) | copy-start | bytes 276484

commit v4 on v3

--- a/solution.py
+++ b/solution.py
@@ -70,11 +70,19 @@
     for axis in BAND:
         bands = bands * lax.axis_size(axis)
     band = lax.axis_index(BAND)
+    held = members * coarse_rows
+    width = own_ref.shape[1]
+    pieces = range(0, columns, width)
+    start = own_ref.shape[0] - held * len(pieces)
     for m in range(members):
         base = m * ext_rows
-        ext_ref[base : base + LSTEPS] = low_ref[m]
-        ext_ref[base + LSTEPS : base + LSTEPS + coarse_rows] = own_ref[m]
-        ext_ref[base + LSTEPS + coarse_rows : base + ext_rows] = high_ref[m]
+        for p, lane in enumerate(pieces):
+            lanes = min(width, columns - lane)
+            at = start + held * p + m * coarse_rows
+            for k, ref in enumerate((low_ref, own_ref, high_ref)):
+                ext_ref[base + coarse_rows * k : base + coarse_rows * (k + 1), lane : lane + lanes] = (
+                    ref[at : at + coarse_rows, :lanes]
+                )
     q = ext_ref[...]
     total = members * ext_rows
     place = lax.rem(lax.broadcasted_iota(jnp.int32, (total, 1), 0), ext_rows)
@@ -109,7 +117,6 @@
     y = jnp.dot(part, kernel_high, preferred_element_type=jnp.float32)
     y = y + jnp.dot(rest, kernel_high, preferred_element_type=jnp.float32)
     y = y + jnp.dot(part, kernel_low_ref[...], preferred_element_type=jnp.float32)
-    held = members * coarse_rows
     blended = jnp.concatenate(
         [y[held * j : held * (j + 1)] for j in range(NLON // BLOCK)], axis=1
     )
@@ -134,49 +141,78 @@
     )(ensemble, low, own, high, kernel_high, kernel_low)
 
 
-def diffuse_body(low_ref, own_ref, high_ref, out_ref, field_ref, east_ref, north_ref):
-    twice, tile_rows, width = own_ref.shape
-    variables = twice // 2
+def diffuse_body(low_ref, own_ref, high_ref, out_ref, stage_ref, field_ref, east_ref, north_ref):
+    variables, tile_rows, _ = out_ref.shape
+    width = own_ref.shape[1]
     height = 3 * tile_rows
+    slots = height // 8
     bands = 1
     for axis in BAND:
         bands = bands * lax.axis_size(axis)
     first = lax.axis_index(BAND) * tile_rows - tile_rows
-    row = first + lax.broadcasted_iota(jnp.int32, (height, 1), 0)
-    inside = (row >= 0) & (row + 1 <= bands * tile_rows - 1)
-    for v in range(variables):
-        field_ref[v] = jnp.concatenate([low_ref[v], own_ref[v], high_ref[v]], axis=0)
-        w = variables + v
-        rate = jnp.concatenate([low_ref[w], own_ref[w], high_ref[w]], axis=0)
-        east_ref[v] = jnp.sqrt(rate * pltpu.roll(rate, width - 1, 1))
-        north_ref[v] = jnp.where(inside, jnp.sqrt(rate * pltpu.roll(rate, height - 1, 0)), 0.0)
-
-    half = SUBSTEPS // 2
-    for low, high in ((0, height), (half, height - half)):
-
-        def substep(_, carry, low=low, high=high):
-            for v in range(variables):
-                f = field_ref[v, low:high]
-                east = east_ref[v, low:high] * (pltpu.roll(f, width - 1, 1) - f)
-                north = north_ref[v, low:high] * (pltpu.roll(f, high - low - 1, 0) - f)
+    sublane = lax.broadcasted_iota(jnp.int32, (8, 1), 0)
+
+    def above(blocks):
+        return blocks[1:] + [pltpu.roll(blocks[0], 7, 0)]
+
+    def below(blocks):
+        return [pltpu.roll(blocks[-1], 1, 0)] + blocks[:-1]
+
+    def interleaved(w):
+        for t in range(width // 128):
+            lanes = slice(128 * t, 128 * (t + 1))
+            for k, ref in enumerate((low_ref, own_ref, high_ref)):
+                stage_ref[t, tile_rows * k : tile_rows * (k + 1)] = ref[
+                    w * tile_rows : (w + 1) * tile_rows, lanes
+                ]
+        return [
+            jnp.concatenate(
+                [stage_ref[t, pl.ds(k, 8, stride=slots)] for t in range(width // 128)], axis=1
+            )
+            for k in range(slots)
+        ]
+
+    for v in range(variables):
+        for k, f in enumerate(interleaved(v)):
+            field_ref[v, k] = f
+        rate = interleaved(variables + v)
+        for k, (own, up) in enumerate(zip(rate, above(rate))):
+            row = first + sublane * slots + k
+            inside = (row >= 0) & (row + 1 <= bands * tile_rows - 1)
+            east_ref[v, k] = jnp.sqrt(own * pltpu.roll(own, width - 1, 1))
+            north_ref[v, k] = jnp.where(inside, jnp.sqrt(own * up), 0.0)
+
+    def substep(_, carry):
+        for v in range(variables):
+            f = [field_ref[v, k] for k in range(slots)]
+            up = above(f)
+            north = [north_ref[v, k] * (up[k] - f[k]) for k in range(slots)]
+            south = below(north)
+            for k in range(slots):
+                east = east_ref[v, k] * (pltpu.roll(f[k], width - 1, 1) - f[k])
                 change = east - pltpu.roll(east, 1, 1)
-                change = change + north - pltpu.roll(north, 1, 0)
-                field_ref[v, low:high] = f + change
-            return carry
-
-        lax.fori_loop(0, half, substep, 0)
-    for v in range(variables):
-        out_ref[v] = field_ref[v, tile_rows : 2 * tile_rows, : out_ref.shape[2]]
-
-
-def diffuse(low, own, high, columns):
-    twice, tile_rows, width = own.shape
-    variables = twice // 2
-    held = pltpu.VMEM((variables, 3 * tile_rows, width), jnp.float32)
+                field_ref[v, k] = f[k] + (change + north[k] - south[k])
+        return carry
+
+    lax.fori_loop(0, SUBSTEPS, substep, 0)
+    for v in range(variables):
+        for t in range(width // 128):
+            for k in range(slots):
+                stage_ref[t, pl.ds(k, 8, stride=slots)] = field_ref[
+                    v, k, :, 128 * t : 128 * (t + 1)
+                ]
+        tile = [stage_ref[t, tile_rows : 2 * tile_rows] for t in range(width // 128)]
+        out_ref[v] = jnp.concatenate(tile, axis=1)[:, : out_ref.shape[2]]
+
+
+def diffuse(low, own, high, shape):
+    variables, tile_rows, columns = shape
+    width = own.shape[1]
+    held = pltpu.VMEM((variables, 3 * tile_rows // 8, 8, width), jnp.float32)
     return pl.pallas_call(
         diffuse_body,
         out_shape=jax.ShapeDtypeStruct((variables, tile_rows, columns), jnp.float32),
-        scratch_shapes=[held, held, held],
+        scratch_shapes=[pltpu.VMEM((width // 128, 3 * tile_rows, 128), jnp.float32), held, held, held],
         compiler_params=params(),
         cost_estimate=pl.CostEstimate(
             flops=16 * 12 * variables * 48 * width, transcendentals=0, bytes_accessed=2 << 20
@@ -185,10 +221,59 @@
     )(low, own, high)
 
 
-def chosen(rows, columns):
-    own = lax.broadcasted_iota(jnp.int32, (rows, columns), 0)
-    other = lax.broadcasted_iota(jnp.int32, (rows, columns), 1)
-    return (own // REFINE == other).astype(jnp.float32)
+def prepare_body(
+    gradient_ref, diffusivity_ref, both_ref, left_ref, right_ref, restricted_ref, sems
+):
+    variables, tile_rows, columns = gradient_ref.shape
+    edge = left_ref.shape[2]
+    reads = [
+        pltpu.make_async_copy(ref, both_ref.at[pl.ds(variables * k, variables)], sems.at[k])
+        for k, ref in enumerate((gradient_ref, diffusivity_ref))
+    ]
+    for read in reads:
+        read.start()
+    for read in reads:
+        read.wait()
+    rows = []
+    for w in range(2 * variables):
+        block = both_ref[w]
+        left_ref[w] = block[:, columns - edge :]
+        right_ref[w] = block[:, :edge]
+    for v in range(variables):
+        for i in range(0, tile_rows, REFINE):
+            rows.append(jnp.sum(both_ref[v, i : i + REFINE], axis=0, keepdims=True))
+    coarse_cols = restricted_ref.shape[1]
+    own = lax.broadcasted_iota(jnp.int32, (columns, coarse_cols), 0)
+    other = lax.broadcasted_iota(jnp.int32, (columns, coarse_cols), 1)
+    chosen = jnp.where(lax.shift_right_logical(own, 2) == other, 1.0, 0.0)
+    total = jnp.dot(
+        jnp.concatenate(rows, axis=0),
+        chosen,
+        precision=lax.Precision.HIGHEST,
+        preferred_element_type=jnp.float32,
+    )
+    restricted_ref[...] = total * (1.0 / (REFINE * REFINE))
+
+
+def prepare(gradient, diffusivity):
+    variables, tile_rows, columns = gradient.shape
+    edge = jax.ShapeDtypeStruct((2 * variables, tile_rows, SUBSTEPS), jnp.float32)
+    return pl.pallas_call(
+        prepare_body,
+        out_shape=(
+            jax.ShapeDtypeStruct((2 * variables, tile_rows, columns), jnp.float32),
+            edge,
+            edge,
+            jax.ShapeDtypeStruct(
+                (variables * tile_rows // REFINE, columns // REFINE), jnp.float32
+            ),
+        ),
+        in_specs=[pl.BlockSpec(memory_space=pltpu.MemorySpace.HBM)] * 2,
+        scratch_shapes=[pltpu.SemaphoreType.DMA((2,))],
+        compiler_params=params(),
+        cost_estimate=pl.CostEstimate(flops=4 << 20, transcendentals=0, bytes_accessed=1 << 20),
+        name="prepare",
+    )(gradient, diffusivity)
 
 
 def combine_body(inverse_count, arrived_ref, smoothed_ref, gradient_ref, direction_ref, sums_ref):
@@ -263,28 +348,29 @@
     members, _, coarse_rows, _ = ensemble.shape
     coarse_cols = columns // REFINE
     owners = lax.axis_size(MEM)
-    row_sums = gradient.reshape(variables * coarse_rows, REFINE, columns).sum(axis=1)
-    restricted = jnp.dot(
-        row_sums, chosen(columns, coarse_cols), precision=lax.Precision.HIGHEST
-    ) * (1.0 / (REFINE * REFINE))
+    both, left, right, restricted = prepare(gradient, diffusivity)
     gathered = everywhere(restricted.reshape(variables, coarse_rows, coarse_cols), MEM)
     gathered = jnp.moveaxis(gathered, 0, 2).reshape(variables, coarse_rows, NLON)
-    both = jnp.concatenate([gradient, diffusivity], axis=0)
-    left = shifted(both[:, :, columns - SUBSTEPS :], MEM, 1)
-    right = shifted(both[:, :, :SUBSTEPS], MEM, -1)
+    left = shifted(left, MEM, 1)
+    right = shifted(right, MEM, -1)
     spare = -(columns + 2 * SUBSTEPS) % 128
     gap = jnp.zeros((2 * variables, tile_rows, spare), jnp.float32)
     extended = jnp.concatenate([both, right, gap, left], axis=2)
+    width = extended.shape[2]
     kernel_high, kernel_low = longitude_kernel()
-    control = jnp.sum(ensemble * gathered[None], axis=1)
-    control_low = shifted(control, BAND, 1)
-    control_high = shifted(control, BAND, -1)
-    rows_low = shifted(extended, BAND, 1)
-    rows_high = shifted(extended, BAND, -1)
-    member_terms = blend(ensemble, control_low, control, control_high, kernel_high, kernel_low)
+    control = jnp.sum(ensemble * gathered[None], axis=1).reshape(members * coarse_rows, NLON)
+    control = jnp.pad(control, ((0, 0), (0, -NLON % width)))
+    own = jnp.concatenate(
+        [extended.reshape(-1, width)]
+        + [control[:, k : k + width] for k in range(0, NLON, width)],
+        axis=0,
+    )
+    low = shifted(own, BAND, 1)
+    high = shifted(own, BAND, -1)
+    member_terms = blend(ensemble, low, own, high, kernel_high, kernel_low)
     blocks = jnp.moveaxis(member_terms.reshape(variables, coarse_rows, owners, coarse_cols), 2, 0)
     arrived = lax.all_to_all(blocks, MEM, split_axis=0, concat_axis=0, tiled=True)
-    smoothed = diffuse(rows_low, extended, rows_high, columns)
+    smoothed = diffuse(low, own, high, gradient.shape)
     peers = lax.axis_size(NEAR)
     direction, sums = combine(
         arrived, smoothed, gradient, 1.0 / (members * owners - 1), peers

time: 101 us -> 112 us (1.11)
  starting transfers between devices: 48.9 us -> 34 us
  blocking collectives: 35.6 us -> 49.3 us
  Pallas kernels: 8.28 us -> 15.5 us
  waiting for transfers between devices: 1.95 us -> 7.88 us
    all_to_all x1, blocking collectives: 20.3 us -> 30.1 us  [shards(): sums = lax.all_to_all(sums, NEAR, split_axis=0, concat_axis=0, tiled=True)]
    ppermute x6 -> x4, starting transfers between devices: 33 us -> 24.4 us  [shifted(): lax.ppermute(block, axis, [(i, (i + step) % count) for i in range(count)])]
    all_to_all x1, waiting for transfers between devices: 0.01 us -> 7.19 us  [everywhere(): return lax.all_to_all(copies, axis, split_axis=0, concat_axis=0, tiled=True)]
    pallas_call x1, Pallas kernels: 5.55 us -> 12.3 us  [diffuse(): pl.pallas_call(diffuse_body, out_shape=jax.ShapeDtypeStruct((variables, t...]
    all_to_all x1, blocking collectives: 15.4 us -> 19.1 us  [everywhere(): return lax.all_to_all(copies, axis, split_axis=0, concat_axis=0, tiled=True)]
    all_to_all x1, starting transfers between devices: 9.26 us -> 6.06 us  [everywhere(): return lax.all_to_all(copies, axis, split_axis=0, concat_axis=0, tiled=True)]
    all_to_all x1, starting transfers between devices: 6.66 us -> 3.51 us  [shards(): lax.all_to_all(blocks, MEM, split_axis=0, concat_axis=0, tiled=True)]
    all_to_all x1, waiting for transfers between devices: 1.93 us -> 0.01 us  [shards(): lax.all_to_all(blocks, MEM, split_axis=0, concat_axis=0, tiled=True)]
  transfers between devices with their start and end apart: 8 -> 6, of which waited for: 1 -> 2; matrix products, arithmetic and copies ran while one was open for 1% -> 1% of each run, Pallas kernels for 7% -> 12%
where the time goes in v4:
time: 112 us; the launch traced here: 111 us
  blocking collectives  49.3 us (44%)
  starting transfers between devices  34 us (30%)
  Pallas kernels  15.5 us (14%)
  waiting for transfers between devices  7.88 us (7%)
  local copies, waits for them, and re-layouts  3.6 us (3%)
    all_to_all x1, blocking collectives, shards(): sums = lax.all_to_all(sums, NEAR, split_axis=0, concat_axis=0, tiled=True)  30.1 us
    ppermute x4, starting transfers between devices, shifted(): lax.ppermute(block, axis, [(i, (i + step) % count) for i in range(count)])  24.4 us
    all_to_all x1, blocking collectives, everywhere(): return lax.all_to_all(copies, axis, split_axis=0, concat_axis=0, tiled=True)  19.1 us
    pallas_call x1, Pallas kernels, diffuse(): pl.pallas_call(diffuse_body, out_shape=jax.ShapeDtypeStruct((variables, t...  12.3 us
    all_to_all x1, waiting for transfers between devices, everywhere(): return lax.all_to_all(copies, axis, split_axis=0, concat_axis=0, tiled=True)  7.19 us
    all_to_all x1, starting transfers between devices, everywhere(): return lax.all_to_all(copies, axis, split_axis=0, concat_axis=0, tiled=True)  6.06 us
    all_to_all x1, starting transfers between devices, shards(): lax.all_to_all(blocks, MEM, split_axis=0, concat_axis=0, tiled=True)  3.51 us
  transfers between devices with their start and end apart: 6, of which 2 were waited for; matrix products, arithmetic and copies ran while one was open for 1% of the time, Pallas kernels for 12%

profile of v4, /device:TPU:1, one launch (start us, length us, event | category | flops | bytes accessed | tf_op | source)
XLA Modules:
  0.0 111.4 jit_solution(13055806335469684910)
XLA Ops:
  0.6 0.0 copy-start.1
  0.6 0.9 copy-done.1
  1.5 0.0 copy-start.3
  1.5 0.9 copy-done.3
  2.4 0.5 prepare.1
  3.0 4.1 %collective-permute-start.1 = (f32[8,16,16]{2,1,0:T(8,128)S(1)}, f32[8,16,16]{2,1,0:T(8,128)S(1)}, u32[]{:S(2)}, u32[]{:S(2)}) collective-permute-start(f32[8,16,16]{2,1,0:T(8,128)S(1)} %get-tuple-element.12), channel_id=1, source_target_pairs={{0,64},{64,128},{128,192},{192,256},{256,320},{320,384},{384,448},... | collective-permute-start | bytes 24584 | tf_op jit(solution)/shard_map/ppermute | solution.py:29
  7.1 5.4 %collective-permute-start = (f32[8,16,16]{2,1,0:T(8,128)S(1)}, f32[8,16,16]{2,1,0:T(8,128)S(1)}, u32[]{:S(2)}, u32[]{:S(2)}) collective-permute-start(f32[8,16,16]{2,1,0:T(8,128)S(1)} %get-tuple-element.11), channel_id=1, source_target_pairs={{0,960},{64,0},{128,64},{192,128},{256,192},{320,256},{384,320},{4... | collective-permute-start | bytes 24584 | tf_op jit(solution)/shard_map/ppermute | solution.py:29
  12.5 0.7 broadcast_in_dim.17
  13.2 6.1 %all-to-all-start = ((f32[16,4,4,90]{3,2,1,0:T(4,128)}), f32[16,4,4,90]{3,2,1,0:T(4,128)S(1)}, u32[]{:S(2)}, u32[]{:S(2)}) async-start(f32[16,4,4,90]{3,2,1,0:T(4,128)} %broadcast_in_dim.17), calls=%async_computation | async-start | bytes 262144 | tf_op jit(solution)/shard_map/all_to_all | solution.py:34
  19.3 0.1 pad.11.clone
  19.4 0.0 collective-permute-done.1
  19.4 0.0 collective-permute-done
  19.4 0.1 pad_maximum_fusion.1
  19.5 0.0 copy-start
  19.5 7.2 %all-to-all-done = f32[16,4,4,90]{3,2,1,0:T(4,128)S(1)} async-done(((f32[16,4,4,90]{3,2,1,0:T(4,128)}), f32[16,4,4,90]{3,2,1,0:T(4,128)S(1)}, u32[]{:S(2)}, u32[]{:S(2)}) %all-to-all-start) | async-done | bytes 92192 | tf_op jit(solution)/shard_map/all_to_all | solution.py:34
  26.7 0.1 mul.10
  26.9 0.0 copy-done
  26.9 0.1 multiply_reduce_fusion
  27.1 7.5 %collective-permute-start.2 = (f32[176,512]{1,0:T(8,128)S(1)}, f32[176,512]{1,0:T(8,128)S(1)}, u32[]{:S(2)}, u32[]{:S(2)}) collective-permute-start(f32[176,512]{1,0:T(8,128)S(1)} %pad_maximum_fusion.own_ref), channel_id=1, source_target_pairs={{0,1},{1,2},{2,3},{3,4},{4,5},{5,6},{6,7},{7,8},{8,9},{9,10},{10,1... | collective-permute-start | bytes 1081352 | tf_op jit(solution)/shard_map/ppermute | solution.py:29
  34.5 7.4 %collective-permute-start.3 = (f32[176,512]{1,0:T(8,128)S(1)}, f32[176,512]{1,0:T(8,128)S(1)}, u32[]{:S(2)}, u32[]{:S(2)}) collective-permute-start(f32[176,512]{1,0:T(8,128)S(1)} %pad_maximum_fusion.own_ref), channel_id=1, source_target_pairs={{0,63},{1,0},{2,1},{3,2},{4,3},{5,4},{6,5},{7,6},{8,7},{9,8},{10,9... | collective-permute-start | bytes 1081352 | tf_op jit(solution)/shard_map/ppermute | solution.py:29
  42.0 0.6 longitude_kernel.1
  42.6 0.0 collective-permute-done.2.low_ref
  42.6 0.7 collective-permute-done.3.high_ref
  43.3 1.1 blend.1
  44.3 0.2 reshape.25
  44.5 0.7 copy.13
  45.2 3.5 %all-to-all-start.1 = ((f32[16,4,4,90]{3,2,1,0:T(4,128)}), f32[16,4,4,90]{3,2,1,0:T(4,128)S(1)}, u32[]{:S(2)}, u32[]{:S(2)}) async-start(f32[16,4,4,90]{3,2,1,0:T(4,128)} %bitcast.11), calls=%async_computation.1 | async-start | bytes 262144 | tf_op jit(solution)/shard_map/all_to_all | solution.py:372
  48.7 0.0 copy-start.2
  48.7 12.3 %diffuse.1.smoothed_ref = f32[4,16,360]{2,1,0:T(8,128)S(1)} custom-call(f32[176,512]{1,0:T(8,128)S(1)} %collective-permute-done.2.low_ref, f32[176,512]{1,0:T(8,128)S(1)} %pad_maximum_fusion.own_ref, f32[176,512]{1,0:T(8,128)S(1)} %collective-permute-done.3.high_ref), custom_call_target="tpu_custom_call" | custom-call | flops 18874368 | bytes 2097152 | tf_op jit(solution)/shard_map/diffuse/pallas_call | solution.py:212
  61.0 0.0 all-to-all-done.1.arrived_ref
  61.0 0.0 copy-done.2
  61.0 0.3 combine.1
  61.3 0.0 copy-start.4
  61.3 30.1 %all_to_all.24 = f32[32,1,128]{2,1,0:T(1,128)S(1)} all-to-all(f32[32,1,128]{2,1,0:T(1,128)S(1)} %bitcast.13), channel_id=1, replica_groups=mesh['mem_0'=2,'mem_1'=8,'band_0'=4,'band_1'=8,'band_2'=2] {'mem_0','mem..., dimensions={0} | all-to-all | bytes 32768 | tf_op jit(solution)/shard_map/all_to_all | solution.py:378
  91.5 0.1 reduce_sum.19
  91.5 19.1 %all_to_all.25 = f32[32,1,128]{2,1,0:T(1,128)S(1)} all-to-all(f32[32,1,128]{2,1,0:T(1,128)S(1)} %broadcast_in_dim.18), channel_id=1, replica_groups=mesh['mem_0'=2,'mem_1'=8,'band_0'=4,'band_1'=8,'band_2'=2] {'band_0','ba..., dimensions={0} | all-to-all | bytes 32768 | tf_op jit(solution)/shard_map/all_to_all | solution.py:34
  110.7 0.0 copy-done.4
  110.7 0.8 step.1
  (6 shorter events, 0.1 us)
Async XLA Ops:
  0.6 0.9 copy-start.1
  1.5 0.9 copy-start.3
  3.0 16.4 %collective-permute-start.1 = (f32[8,16,16]{2,1,0:T(8,128)S(1)}, f32[8,16,16]{2,1,0:T(8,128)S(1)}, u32[]{:S(2)}, u32[]{:S(2)}) collective-permute-start(f32[8,16,16]{2,1,0:T(8,128)S(1)} %get-tuple-element.12), channel_id=1, source_target_pairs={{0,64},{64,128},{128,192},{192,256},{256,320},{320,384},{384,448},... | collective-permute-start | bytes 24584 | tf_op jit(solution)/shard_map/ppermute | solution.py:29
  7.1 12.2 %collective-permute-start = (f32[8,16,16]{2,1,0:T(8,128)S(1)}, f32[8,16,16]{2,1,0:T(8,128)S(1)}, u32[]{:S(2)}, u32[]{:S(2)}) collective-permute-start(f32[8,16,16]{2,1,0:T(8,128)S(1)} %get-tuple-element.11), channel_id=1, source_target_pairs={{0,960},{64,0},{128,64},{192,128},{256,192},{320,256},{384,320},{4... | collective-permute-start | bytes 24584 | tf_op jit(solution)/shard_map/ppermute | solution.py:29
  13.2 13.5 %all-to-all-start = ((f32[16,4,4,90]{3,2,1,0:T(4,128)}), f32[16,4,4,90]{3,2,1,0:T(4,128)S(1)}, u32[]{:S(2)}, u32[]{:S(2)}) async-start(f32[16,4,4,90]{3,2,1,0:T(4,128)} %broadcast_in_dim.17), calls=%async_computation | async-start | bytes 262144 | tf_op jit(solution)/shard_map/all_to_all | solution.py:34
  19.5 7.4 %copy-start = (f32[4,4,4,1440]{3,2,1,0:T(4,128)S(1)}, f32[4,4,4,1440]{3,2,1,0:T(4,128)}, u32[]{:S(2)}) copy-start(f32[4,4,4,1440]{3,2,1,0:T(4,128)} %ensemble_ref.1) | copy-start | bytes 1105924
  27.1 15.5 %collective-permute-start.2 = (f32[176,512]{1,0:T(8,128)S(1)}, f32[176,512]{1,0:T(8,128)S(1)}, u32[]{:S(2)}, u32[]{:S(2)}) collective-permute-start(f32[176,512]{1,0:T(8,128)S(1)} %pad_maximum_fusion.own_ref), channel_id=1, source_target_pairs={{0,1},{1,2},{2,3},{3,4},{4,5},{5,6},{6,7},{7,8},{8,9},{9,10},{10,1... | collective-permute-start | bytes 1081352 | tf_op jit(solution)/shard_map/ppermute | solution.py:29
  34.5 8.7 %collective-permute-start.3 = (f32[176,512]{1,0:T(8,128)S(1)}, f32[176,512]{1,0:T(8,128)S(1)}, u32[]{:S(2)}, u32[]{:S(2)}) collective-permute-start(f32[176,512]{1,0:T(8,128)S(1)} %pad_maximum_fusion.own_ref), channel_id=1, source_target_pairs={{0,63},{1,0},{2,1},{3,2},{4,3},{5,4},{6,5},{7,6},{8,7},{9,8},{10,9... | collective-permute-start | bytes 1081352 | tf_op jit(solution)/shard_map/ppermute | solution.py:29
  45.2 15.8 %all-to-all-start.1 = ((f32[16,4,4,90]{3,2,1,0:T(4,128)}), f32[16,4,4,90]{3,2,1,0:T(4,128)S(1)}, u32[]{:S(2)}, u32[]{:S(2)}) async-start(f32[16,4,4,90]{3,2,1,0:T(4,128)} %bitcast.11), calls=%async_computation.1 | async-start | bytes 262144 | tf_op jit(solution)/shard_map/all_to_all | solution.py:372
  48.7 12.3 %copy-start.2 = (f32[4,16,360]{2,1,0:T(8,128)S(1)}, f32[4,16,360]{2,1,0:T(8,128)}, u32[]{:S(2)}) copy-start(f32[4,16,360]{2,1,0:T(8,128)} %gradient_ref.3) | copy-start | bytes 276484
  61.3 49.4 %copy-start.4 = (f32[4,16,360]{2,1,0:T(8,128)S(1)}, f32[4,16,360]{2,1,0:T(8,128)}, u32[]{:S(2)}) copy-start(f32[4,16,360]{2,1,0:T(8,128)} %previous_ref.1) | copy-start | bytes 276484

commit v5 on v3

--- a/solution.py
+++ b/solution.py
@@ -7,6 +7,7 @@
 from jax.experimental.pallas import tpu as pltpu
 from jax.sharding import Mesh
 from jax.sharding import PartitionSpec as P
+
 
 NLON = 1440
 REFINE = 4
@@ -24,9 +25,14 @@
 VMEM_LIMIT = 24 << 20
 
 
-def shifted(block, axis, step):
+def swapped(block, axis, odd):
     count = lax.axis_size(axis)
-    return lax.ppermute(block, axis, [(i, (i + step) % count) for i in range(count)])
+    pairs = [(i, ((i + odd) ^ 1) - odd) for i in range(count)]
+    return lax.ppermute(block, axis, [(i, partner % count) for i, partner in pairs])
+
+
+def is_even(axis):
+    return lax.rem(lax.axis_index(axis), 2) == 0
 
 
 def everywhere(shard, axis):
@@ -63,18 +69,20 @@
     )()
 
 
-def blend_body(ensemble_ref, low_ref, own_ref, high_ref, kernel_high_ref, kernel_low_ref, out_ref, ext_ref):
-    members, variables, coarse_rows, columns = ensemble_ref.shape
+def blend_body(ensemble_ref, near_ref, own_ref, far_ref, kernel_high_ref, kernel_low_ref, out_ref, ext_ref):
+    members, variables, coarse_rows, _ = ensemble_ref.shape
     ext_rows = coarse_rows + 2 * LSTEPS
     bands = 1
     for axis in BAND:
         bands = bands * lax.axis_size(axis)
     band = lax.axis_index(BAND)
+    even = lax.rem(band, 2) == 0
     for m in range(members):
         base = m * ext_rows
-        ext_ref[base : base + LSTEPS] = low_ref[m]
+        near, far = near_ref[m], far_ref[m]
+        ext_ref[base : base + LSTEPS] = jnp.where(even, far, near)
         ext_ref[base + LSTEPS : base + LSTEPS + coarse_rows] = own_ref[m]
-        ext_ref[base + LSTEPS + coarse_rows : base + ext_rows] = high_ref[m]
+        ext_ref[base + LSTEPS + coarse_rows : base + ext_rows] = jnp.where(even, near, far)
     q = ext_ref[...]
     total = members * ext_rows
     place = lax.rem(lax.broadcasted_iota(jnp.int32, (total, 1), 0), ext_rows)
@@ -120,7 +128,7 @@
         out_ref[v] = term
 
 
-def blend(ensemble, low, own, high, kernel_high, kernel_low):
+def blend(ensemble, near, own, far, kernel_high, kernel_low):
     members, variables, coarse_rows, columns = ensemble.shape
     return pl.pallas_call(
         blend_body,
@@ -131,23 +139,29 @@
             flops=6 * 16 * NLON * NLON, transcendentals=0, bytes_accessed=4 << 20
         ),
         name="blend",
-    )(ensemble, low, own, high, kernel_high, kernel_low)
-
-
-def diffuse_body(low_ref, own_ref, high_ref, out_ref, field_ref, east_ref, north_ref):
+    )(ensemble, near, own, far, kernel_high, kernel_low)
+
+
+def diffuse_body(near_ref, own_ref, far_ref, out_ref, field_ref, east_ref, north_ref):
     twice, tile_rows, width = own_ref.shape
     variables = twice // 2
     height = 3 * tile_rows
     bands = 1
     for axis in BAND:
         bands = bands * lax.axis_size(axis)
+    even = is_even(BAND)
     first = lax.axis_index(BAND) * tile_rows - tile_rows
+
+    def stacked(w):
+        near, far = near_ref[w], far_ref[w]
+        below, above = jnp.where(even, far, near), jnp.where(even, near, far)
+        return jnp.concatenate([below, own_ref[w], above], axis=0)
+
     row = first + lax.broadcasted_iota(jnp.int32, (height, 1), 0)
     inside = (row >= 0) & (row + 1 <= bands * tile_rows - 1)
     for v in range(variables):
-        field_ref[v] = jnp.concatenate([low_ref[v], own_ref[v], high_ref[v]], axis=0)
-        w = variables + v
-        rate = jnp.concatenate([low_ref[w], own_ref[w], high_ref[w]], axis=0)
+        field_ref[v] = stacked(v)
+        rate = stacked(variables + v)
         east_ref[v] = jnp.sqrt(rate * pltpu.roll(rate, width - 1, 1))
         north_ref[v] = jnp.where(inside, jnp.sqrt(rate * pltpu.roll(rate, height - 1, 0)), 0.0)
 
@@ -169,7 +183,7 @@
         out_ref[v] = field_ref[v, tile_rows : 2 * tile_rows, : out_ref.shape[2]]
 
 
-def diffuse(low, own, high, columns):
+def diffuse(near, own, far, columns):
     twice, tile_rows, width = own.shape
     variables = twice // 2
     held = pltpu.VMEM((variables, 3 * tile_rows, width), jnp.float32)
@@ -182,7 +196,7 @@
             flops=16 * 12 * variables * 48 * width, transcendentals=0, bytes_accessed=2 << 20
         ),
         name="diffuse",
-    )(low, own, high)
+    )(near, own, far)
 
 
 def chosen(rows, columns):
@@ -267,24 +281,31 @@
     restricted = jnp.dot(
         row_sums, chosen(columns, coarse_cols), precision=lax.Precision.HIGHEST
     ) * (1.0 / (REFINE * REFINE))
-    gathered = everywhere(restricted.reshape(variables, coarse_rows, coarse_cols), MEM)
+    payload = jnp.broadcast_to(
+        restricted.reshape(1, variables, coarse_rows, coarse_cols),
+        (owners, variables, coarse_rows, coarse_cols),
+    )
+    both = jnp.concatenate([gradient, diffusivity], axis=0)
+    even = is_even(MEM)
+    first, last = both[:, :, :SUBSTEPS], both[:, :, columns - SUBSTEPS :]
+    up, down = jnp.where(even, last, first), jnp.where(even, first, last)
+    gathered = lax.all_to_all(payload, MEM, split_axis=0, concat_axis=0, tiled=True)
     gathered = jnp.moveaxis(gathered, 0, 2).reshape(variables, coarse_rows, NLON)
-    both = jnp.concatenate([gradient, diffusivity], axis=0)
-    left = shifted(both[:, :, columns - SUBSTEPS :], MEM, 1)
-    right = shifted(both[:, :, :SUBSTEPS], MEM, -1)
+    up, down = swapped(up, MEM, 0), swapped(down, MEM, 1)
+    left, right = jnp.where(even, down, up), jnp.where(even, up, down)
     spare = -(columns + 2 * SUBSTEPS) % 128
     gap = jnp.zeros((2 * variables, tile_rows, spare), jnp.float32)
     extended = jnp.concatenate([both, right, gap, left], axis=2)
     kernel_high, kernel_low = longitude_kernel()
     control = jnp.sum(ensemble * gathered[None], axis=1)
-    control_low = shifted(control, BAND, 1)
-    control_high = shifted(control, BAND, -1)
-    rows_low = shifted(extended, BAND, 1)
-    rows_high = shifted(extended, BAND, -1)
-    member_terms = blend(ensemble, control_low, control, control_high, kernel_high, kernel_low)
+    control_near = swapped(control, BAND, 0)
+    control_far = swapped(control, BAND, 1)
+    rows_near = swapped(extended, BAND, 0)
+    rows_far = swapped(extended, BAND, 1)
+    member_terms = blend(ensemble, control_near, control, control_far, kernel_high, kernel_low)
     blocks = jnp.moveaxis(member_terms.reshape(variables, coarse_rows, owners, coarse_cols), 2, 0)
     arrived = lax.all_to_all(blocks, MEM, split_axis=0, concat_axis=0, tiled=True)
-    smoothed = diffuse(rows_low, extended, rows_high, columns)
+    smoothed = diffuse(rows_near, extended, rows_far, columns)
     peers = lax.axis_size(NEAR)
     direction, sums = combine(
         arrived, smoothed, gradient, 1.0 / (members * owners - 1), peers

time: 101 us -> 100 us (0.990)
  waiting for transfers between devices: 1.95 us -> 9.14 us
  starting transfers between devices: 48.9 us -> 45.4 us
  blocking collectives: 35.6 us -> 32.5 us
    all_to_all x1, waiting for transfers between devices: 0.01 us -> 7.24 us  [shards(): lax.all_to_all(payload, MEM, split_axis=0, concat_axis=0, tiled=True)]
    all_to_all x1, starting transfers between devices: 9.26 us -> 3.51 us  [shards(): lax.all_to_all(payload, MEM, split_axis=0, concat_axis=0, tiled=True)]
    ppermute x6, starting transfers between devices: 33 us -> 38.4 us  [swapped(): lax.ppermute(block, axis, [(i, partner % count) for i, partner in pairs])]
    all_to_all x1, blocking collectives: 20.3 us -> 16 us  [shards(): sums = lax.all_to_all(sums, NEAR, split_axis=0, concat_axis=0, tiled=True)]
    all_to_all x1, starting transfers between devices: 6.66 us -> 3.51 us  [shards(): lax.all_to_all(blocks, MEM, split_axis=0, concat_axis=0, tiled=True)]
    all_to_all x1, blocking collectives: 15.4 us -> 16.5 us  [everywhere(): return lax.all_to_all(copies, axis, split_axis=0, concat_axis=0, tiled=True)]
  transfers between devices with their start and end apart: 8 -> 8, of which waited for: 1 -> 2; matrix products, arithmetic and copies ran while one was open for 1% -> 2% of each run, Pallas kernels for 7% -> 7%
where the time goes in v5:
time: 100 us; the launch traced here: 99.8 us
  starting transfers between devices  45.4 us (45%)
  blocking collectives  32.5 us (32%)
  waiting for transfers between devices  9.14 us (9%)
  Pallas kernels  8.33 us (8%)
  local copies, waits for them, and re-layouts  2.78 us (3%)
    ppermute x6, starting transfers between devices, swapped(): lax.ppermute(block, axis, [(i, partner % count) for i, partner in pairs])  38.4 us
    all_to_all x1, blocking collectives, everywhere(): return lax.all_to_all(copies, axis, split_axis=0, concat_axis=0, tiled=True)  16.5 us
    all_to_all x1, blocking collectives, shards(): sums = lax.all_to_all(sums, NEAR, split_axis=0, concat_axis=0, tiled=True)  16 us
    all_to_all x1, waiting for transfers between devices, shards(): lax.all_to_all(payload, MEM, split_axis=0, concat_axis=0, tiled=True)  7.24 us
    pallas_call x1, Pallas kernels, diffuse(): pl.pallas_call(diffuse_body, out_shape=jax.ShapeDtypeStruct((variables, t...  5.58 us
    all_to_all x1, starting transfers between devices, shards(): lax.all_to_all(payload, MEM, split_axis=0, concat_axis=0, tiled=True)  3.51 us
    all_to_all x1, starting transfers between devices, shards(): lax.all_to_all(blocks, MEM, split_axis=0, concat_axis=0, tiled=True)  3.51 us
  transfers between devices with their start and end apart: 8, of which 2 were waited for; matrix products, arithmetic and copies ran while one was open for 2% of the time, Pallas kernels for 7%

profile of v5, /device:TPU:1, one launch (start us, length us, event | category | flops | bytes accessed | tf_op | source)
XLA Modules:
  0.0 99.8 jit_solution(13299419789181837274)
XLA Ops:
  0.6 0.0 copy-start.3
  0.6 0.9 constant_dynamic-update-slice_fusion.1
  1.6 0.0 copy-done.3
  1.6 0.0 copy-start.1
  1.6 0.1 slice_select_fusion.1
  1.7 4.1 %collective-permute-start.2 = (f32[8,16,16]{2,1,0:T(8,128)S(1)}, f32[8,16,16]{2,1,0:T(8,128)S(1)}, u32[]{:S(2)}, u32[]{:S(2)}) collective-permute-start(f32[8,16,16]{2,1,0:T(8,128)S(1)} %get-tuple-element.10), channel_id=1, source_target_pairs={{0,64},{64,0},{128,192},{192,128},{256,320},{320,256},{384,448},{4... | collective-permute-start | bytes 24584 | tf_op jit(solution)/shard_map/ppermute | solution.py:31
  5.8 6.4 %collective-permute-start.3 = (f32[8,16,16]{2,1,0:T(8,128)S(1)}, f32[8,16,16]{2,1,0:T(8,128)S(1)}, u32[]{:S(2)}, u32[]{:S(2)}) collective-permute-start(f32[8,16,16]{2,1,0:T(8,128)S(1)} %get-tuple-element.11), channel_id=1, source_target_pairs={{0,960},{64,128},{128,64},{192,256},{256,192},{320,384},{384,320},... | collective-permute-start | bytes 24584 | tf_op jit(solution)/shard_map/ppermute | solution.py:31
  12.2 0.0 copy-done.1
  12.3 0.1 reduce_sum.27
  12.4 0.4 convolution_multiply_fusion
  12.7 0.7 broadcast_in_dim.16
  13.4 3.5 %all-to-all-start = ((f32[16,4,4,90]{3,2,1,0:T(4,128)}), f32[16,4,4,90]{3,2,1,0:T(4,128)S(1)}, u32[]{:S(2)}, u32[]{:S(2)}) async-start(f32[16,4,4,90]{3,2,1,0:T(4,128)} %broadcast_in_dim.16), calls=%async_computation | async-start | bytes 262144 | tf_op jit(solution)/shard_map/all_to_all | solution.py:292
  16.9 0.0 copy-start
  16.9 0.1 pad.2.clone
  17.0 0.0 collective-permute-done.2
  17.0 0.0 collective-permute-done.3
  17.0 7.2 %all-to-all-done = f32[16,4,4,90]{3,2,1,0:T(4,128)S(1)} async-done(((f32[16,4,4,90]{3,2,1,0:T(4,128)}), f32[16,4,4,90]{3,2,1,0:T(4,128)S(1)}, u32[]{:S(2)}, u32[]{:S(2)}) %all-to-all-start) | async-done | bytes 92192 | tf_op jit(solution)/shard_map/all_to_all | solution.py:292
  24.3 0.1 mul.21
  24.5 0.0 copy-done
  24.5 0.1 multiply_reduce_fusion.own_ref
  24.6 12.6 %collective-permute-start = (f32[4,4,1440]{2,1,0:T(4,128)S(1)}, f32[4,4,1440]{2,1,0:T(4,128)S(1)}, u32[]{:S(2)}, u32[]{:S(2)}) collective-permute-start(f32[4,4,1440]{2,1,0:T(4,128)S(1)} %multiply_reduce_fusion.own_ref), channel_id=1, source_target_pairs={{0,1},{1,0},{2,3},{3,2},{4,5},{5,4},{6,7},{7,6},{8,9},{9,8},{10,11... | collective-permute-start | bytes 276488 | tf_op jit(solution)/shard_map/ppermute | solution.py:31
  37.1 1.9 %collective-permute-start.1 = (f32[4,4,1440]{2,1,0:T(4,128)S(1)}, f32[4,4,1440]{2,1,0:T(4,128)S(1)}, u32[]{:S(2)}, u32[]{:S(2)}) collective-permute-start(f32[4,4,1440]{2,1,0:T(4,128)S(1)} %multiply_reduce_fusion.own_ref), channel_id=1, source_target_pairs={{0,63},{1,2},{2,1},{3,4},{4,3},{5,6},{6,5},{7,8},{8,7},{9,10},{10,... | collective-permute-start | bytes 276488 | tf_op jit(solution)/shard_map/ppermute | solution.py:31
  39.1 0.1 pad_maximum_fusion.own_ref
  39.2 11.5 %collective-permute-start.4 = (f32[8,16,512]{2,1,0:T(8,128)S(1)}, f32[8,16,512]{2,1,0:T(8,128)S(1)}, u32[]{:S(2)}, u32[]{:S(2)}) collective-permute-start(f32[8,16,512]{2,1,0:T(8,128)S(1)} %pad_maximum_fusion.own_ref), channel_id=1, source_target_pairs={{0,1},{1,0},{2,3},{3,2},{4,5},{5,4},{6,7},{7,6},{8,9},{9,8},{10,11... | collective-permute-start | bytes 786440 | tf_op jit(solution)/shard_map/ppermute | solution.py:31
  50.7 1.9 %collective-permute-start.5 = (f32[8,16,512]{2,1,0:T(8,128)S(1)}, f32[8,16,512]{2,1,0:T(8,128)S(1)}, u32[]{:S(2)}, u32[]{:S(2)}) collective-permute-start(f32[8,16,512]{2,1,0:T(8,128)S(1)} %pad_maximum_fusion.own_ref), channel_id=1, source_target_pairs={{0,63},{1,2},{2,1},{3,4},{4,3},{5,6},{6,5},{7,8},{8,7},{9,10},{10,... | collective-permute-start | bytes 786440 | tf_op jit(solution)/shard_map/ppermute | solution.py:31
  52.6 0.6 longitude_kernel.1
  53.2 0.0 collective-permute-done.near_ref
  53.2 0.0 collective-permute-done.1.far_ref
  53.2 1.1 %blend.1 = f32[4,4,1440]{2,1,0:T(4,128)S(1)} custom-call(f32[4,4,4,1440]{3,2,1,0:T(4,128)S(1)} %copy-done, f32[4,4,1440]{2,1,0:T(4,128)S(1)} %collective-permute-done.near_ref, f32[4,4,1440]{2,1,0:T(4,128)S(1)} %multiply_reduce_fusion.own_ref, f32[4,4,1440]{2,1,0:T(4,128)S(1)} %collective-permute-done.1.far_ref, ...), custom_call_target="tpu_custom_call" | custom-call | flops 199065600 | bytes 4194304 | tf_op jit(solution)/shard_map/blend/pallas_call | solution.py:133
  54.3 0.2 reshape.22
  54.5 0.7 copy.13
  55.2 3.5 %all-to-all-start.1 = ((f32[16,4,4,90]{3,2,1,0:T(4,128)}), f32[16,4,4,90]{3,2,1,0:T(4,128)S(1)}, u32[]{:S(2)}, u32[]{:S(2)}) async-start(f32[16,4,4,90]{3,2,1,0:T(4,128)} %bitcast.11), calls=%async_computation.1 | async-start | bytes 262144 | tf_op jit(solution)/shard_map/all_to_all | solution.py:307
  58.7 0.0 collective-permute-done.4.near_ref
  58.7 0.0 collective-permute-done.5.far_ref
  58.7 5.6 %diffuse.1.smoothed_ref = f32[4,16,360]{2,1,0:T(8,128)S(1)} custom-call(f32[8,16,512]{2,1,0:T(8,128)S(1)} %collective-permute-done.4.near_ref, f32[8,16,512]{2,1,0:T(8,128)S(1)} %pad_maximum_fusion.own_ref, f32[8,16,512]{2,1,0:T(8,128)S(1)} %collective-permute-done.5.far_ref), custom_call_target="tpu_custom_call" | custom-call | flops 18874368 | bytes 2097152 | tf_op jit(solution)/shard_map/diffuse/pallas_call | solution.py:190
  64.3 1.9 %all-to-all-done.1.arrived_ref = f32[16,4,4,90]{3,2,1,0:T(4,128)S(1)} async-done(((f32[16,4,4,90]{3,2,1,0:T(4,128)}), f32[16,4,4,90]{3,2,1,0:T(4,128)S(1)}, u32[]{:S(2)}, u32[]{:S(2)}) %all-to-all-start.1) | async-done | bytes 92192 | tf_op jit(solution)/shard_map/all_to_all | solution.py:307
  66.2 0.3 combine.1
  66.5 0.0 copy-start.2
  66.5 16.0 %all_to_all.24 = f32[32,1,128]{2,1,0:T(1,128)S(1)} all-to-all(f32[32,1,128]{2,1,0:T(1,128)S(1)} %bitcast.13), channel_id=1, replica_groups=mesh['mem_0'=2,'mem_1'=8,'band_0'=4,'band_1'=8,'band_2'=2] {'mem_0','mem..., dimensions={0} | all-to-all | bytes 32768 | tf_op jit(solution)/shard_map/all_to_all | solution.py:313
  82.5 0.1 reduce_sum.29
  82.6 16.5 %all_to_all.25 = f32[32,1,128]{2,1,0:T(1,128)S(1)} all-to-all(f32[32,1,128]{2,1,0:T(1,128)S(1)} %broadcast_in_dim.18), channel_id=1, replica_groups=mesh['mem_0'=2,'mem_1'=8,'band_0'=4,'band_1'=8,'band_2'=2] {'band_0','ba..., dimensions={0} | all-to-all | bytes 32768 | tf_op jit(solution)/shard_map/all_to_all | solution.py:40
  99.0 0.0 copy-done.2
  99.0 0.8 step.1
  (8 shorter events, 0.1 us)
Async XLA Ops:
  0.6 0.9 copy-start.3
  1.6 10.6 %copy-start.1 = (f32[4,16,360]{2,1,0:T(8,128)S(1)}, f32[4,16,360]{2,1,0:T(8,128)}, u32[]{:S(2)}) copy-start(f32[4,16,360]{2,1,0:T(8,128)} %gradient_ref.1) | copy-start | bytes 276484
  1.7 15.3 %collective-permute-start.2 = (f32[8,16,16]{2,1,0:T(8,128)S(1)}, f32[8,16,16]{2,1,0:T(8,128)S(1)}, u32[]{:S(2)}, u32[]{:S(2)}) collective-permute-start(f32[8,16,16]{2,1,0:T(8,128)S(1)} %get-tuple-element.10), channel_id=1, source_target_pairs={{0,64},{64,0},{128,192},{192,128},{256,320},{320,256},{384,448},{4... | collective-permute-start | bytes 24584 | tf_op jit(solution)/shard_map/ppermute | solution.py:31
  5.8 11.2 %collective-permute-start.3 = (f32[8,16,16]{2,1,0:T(8,128)S(1)}, f32[8,16,16]{2,1,0:T(8,128)S(1)}, u32[]{:S(2)}, u32[]{:S(2)}) collective-permute-start(f32[8,16,16]{2,1,0:T(8,128)S(1)} %get-tuple-element.11), channel_id=1, source_target_pairs={{0,960},{64,128},{128,64},{192,256},{256,192},{320,384},{384,320},... | collective-permute-start | bytes 24584 | tf_op jit(solution)/shard_map/ppermute | solution.py:31
  13.4 10.9 %all-to-all-start = ((f32[16,4,4,90]{3,2,1,0:T(4,128)}), f32[16,4,4,90]{3,2,1,0:T(4,128)S(1)}, u32[]{:S(2)}, u32[]{:S(2)}) async-start(f32[16,4,4,90]{3,2,1,0:T(4,128)} %broadcast_in_dim.16), calls=%async_computation | async-start | bytes 262144 | tf_op jit(solution)/shard_map/all_to_all | solution.py:292
  16.9 7.5 %copy-start = (f32[4,4,4,1440]{3,2,1,0:T(4,128)S(1)}, f32[4,4,4,1440]{3,2,1,0:T(4,128)}, u32[]{:S(2)}) copy-start(f32[4,4,4,1440]{3,2,1,0:T(4,128)} %ensemble_ref.1) | copy-start | bytes 1105924
  24.6 28.7 %collective-permute-start = (f32[4,4,1440]{2,1,0:T(4,128)S(1)}, f32[4,4,1440]{2,1,0:T(4,128)S(1)}, u32[]{:S(2)}, u32[]{:S(2)}) collective-permute-start(f32[4,4,1440]{2,1,0:T(4,128)S(1)} %multiply_reduce_fusion.own_ref), channel_id=1, source_target_pairs={{0,1},{1,0},{2,3},{3,2},{4,5},{5,4},{6,7},{7,6},{8,9},{9,8},{10,11... | collective-permute-start | bytes 276488 | tf_op jit(solution)/shard_map/ppermute | solution.py:31
  37.1 16.1 %collective-permute-start.1 = (f32[4,4,1440]{2,1,0:T(4,128)S(1)}, f32[4,4,1440]{2,1,0:T(4,128)S(1)}, u32[]{:S(2)}, u32[]{:S(2)}) collective-permute-start(f32[4,4,1440]{2,1,0:T(4,128)S(1)} %multiply_reduce_fusion.own_ref), channel_id=1, source_target_pairs={{0,63},{1,2},{2,1},{3,4},{4,3},{5,6},{6,5},{7,8},{8,7},{9,10},{10,... | collective-permute-start | bytes 276488 | tf_op jit(solution)/shard_map/ppermute | solution.py:31
  39.2 19.5 %collective-permute-start.4 = (f32[8,16,512]{2,1,0:T(8,128)S(1)}, f32[8,16,512]{2,1,0:T(8,128)S(1)}, u32[]{:S(2)}, u32[]{:S(2)}) collective-permute-start(f32[8,16,512]{2,1,0:T(8,128)S(1)} %pad_maximum_fusion.own_ref), channel_id=1, source_target_pairs={{0,1},{1,0},{2,3},{3,2},{4,5},{5,4},{6,7},{7,6},{8,9},{9,8},{10,11... | collective-permute-start | bytes 786440 | tf_op jit(solution)/shard_map/ppermute | solution.py:31
  50.7 8.0 %collective-permute-start.5 = (f32[8,16,512]{2,1,0:T(8,128)S(1)}, f32[8,16,512]{2,1,0:T(8,128)S(1)}, u32[]{:S(2)}, u32[]{:S(2)}) collective-permute-start(f32[8,16,512]{2,1,0:T(8,128)S(1)} %pad_maximum_fusion.own_ref), channel_id=1, source_target_pairs={{0,63},{1,2},{2,1},{3,4},{4,3},{5,6},{6,5},{7,8},{8,7},{9,10},{10,... | collective-permute-start | bytes 786440 | tf_op jit(solution)/shard_map/ppermute | solution.py:31
  55.2 11.0 %all-to-all-start.1 = ((f32[16,4,4,90]{3,2,1,0:T(4,128)}), f32[16,4,4,90]{3,2,1,0:T(4,128)S(1)}, u32[]{:S(2)}, u32[]{:S(2)}) async-start(f32[16,4,4,90]{3,2,1,0:T(4,128)} %bitcast.11), calls=%async_computation.1 | async-start | bytes 262144 | tf_op jit(solution)/shard_map/all_to_all | solution.py:307
  66.5 32.6 %copy-start.2 = (f32[4,16,360]{2,1,0:T(8,128)S(1)}, f32[4,16,360]{2,1,0:T(8,128)}, u32[]{:S(2)}) copy-start(f32[4,16,360]{2,1,0:T(8,128)} %previous_ref.1) | copy-start | bytes 276484
